TPU v7x, 32 devices: a whole 2x2x4 slice. The times are simulated.
32 devices in a mesh: pole: 4 (over x, core), row: 4 (over z), col: 2 (over y).
Axes of the slice: x: 2, y: 2, z: 4, core: 2. Of those that a mesh axis runs over, the one named last changes fastest.
Arguments:
- anc_inverse: bfloat16 [4, 2, 4, 192, 768], P('pole', None, None, 'col', 'row'), may hold values from -6 to 6
- panel: bfloat16 [4, 2, 768, 1024], P('pole', None, ('row', 'col')), may hold values from -0.21875 to 0.21875
- pattern: int32 [8, 2], replicated, may hold values 0 or 1
- diag_inverse: bfloat16 [4, 2, 1024, 512], P('pole', None, 'col', 'row'), may hold values from -6 to 6
- pole_weights: float32 [4, 2], P('pole'), may hold values from -4 to 4
Outputs:
- inv_panel: float32 [4, 2, 768, 1024], P('pole', None, 'row', 'col')
- inv_diag: bfloat16 [4, 2, 1024, 512], P('pole', None, 'col', 'row')
- density: float32 [1024, 512], P('col', 'row')
All inputs are finite; a program needn't handle non-finite values.
Results may differ from a plain program's by a relative error of at most 0.013.
Values may be sent and summed in bfloat16 or wider, within the bound.
No kernel may reach another device: no remote copies, remote signals or barrier semaphores. Data moves between devices by JAX's collectives and lax.ppermute only.
A program may use at most 128 MiB of HBM per device.

v0:
```python
import jax
import jax.numpy as jnp
from jax import lax
from jax.sharding import PartitionSpec as P


def complex_left(left_re, left_im, right_re, right_im):
    upper = jnp.concatenate([left_re, left_im], axis=1)
    lower = jnp.concatenate([-left_im, left_re], axis=1)
    left_side = jnp.concatenate([upper, lower], axis=0)
    right_side = jnp.concatenate([right_re, right_im], axis=0)
    product = lax.dot_general(
        left_side, right_side, (((0,), (0,)), ((), ())), preferred_element_type=jnp.float32
    )
    return product.reshape(2, left_re.shape[1], right_re.shape[1])


def body(anc_inverse, panel, pattern, diag_inverse, pole_weights):
    n_row = lax.axis_size("row")
    n_col = lax.axis_size("col")
    fine_block = lax.axis_index("row") * n_col + lax.axis_index("col")
    pattern_row = lax.dynamic_slice_in_dim(pattern, fine_block, 1, 0)
    block_rows = panel.shape[2]
    width_all = panel.shape[3]
    groups = pattern.shape[1]
    keep_mask = pattern_row.astype(jnp.bfloat16).reshape(1, 1, 1, groups, 1)
    masked = (panel.reshape(1, 2, block_rows, groups, width_all // groups) * keep_mask).reshape(
        1, 2, block_rows, width_all
    )
    local_rows = lax.all_to_all(masked, "col", split_axis=3, concat_axis=2, tiled=True)
    row_count = anc_inverse.shape[4]
    col_count = local_rows.shape[3]
    full_cols = lax.all_gather(local_rows, "row", axis=2, tiled=True)
    stacked = full_cols[0].reshape(2, n_row, block_rows * n_col, col_count)
    segment = lax.all_gather(anc_inverse, "col", axis=3, tiled=True)
    length = segment.shape[3]
    left_side = segment[0].reshape(2, n_row * length, row_count)
    right_side = stacked.reshape(2, n_row * length, col_count)
    summed = complex_left(left_side[0], left_side[1], right_side[0], right_side[1])
    result_panel = -summed
    rounded = result_panel.astype(jnp.bfloat16)
    diag_terms = complex_left(local_rows[0, 0], local_rows[0, 1], rounded[0], rounded[1])
    row_share = lax.psum_scatter(diag_terms, "row", scatter_dimension=2, tiled=True)
    inverse_diag = diag_inverse[0].astype(jnp.float32) - row_share
    pole_weight = pole_weights[0]
    density_term = pole_weight[0] * inverse_diag[1] + pole_weight[1] * inverse_diag[0]
    density = lax.psum(density_term.astype(jnp.bfloat16), "pole").astype(jnp.float32)
    return (result_panel[None], inverse_diag.astype(jnp.bfloat16)[None], density)


def solution(mesh):
    placed = (
        P("pole", None, None, "col", "row"),
        P("pole", None, ("row", "col"), None),
        P(),
        P("pole", None, "col", "row"),
        P("pole", None),
    )
    return jax.shard_map(
        body,
        mesh=mesh,
        in_specs=placed,
        out_specs=(P("pole", None, "row", "col"), P("pole", None, "col", "row"), P("col", "row")),
        check_vma=False,
    )
```

profile of v0, /device:TPU:0, one launch (start us, length us, event | category | flops | bytes accessed | tf_op | source)
XLA Modules:
  0.0 151.4 jit_solution(4732061525736366362)
XLA Ops:
  7.2 0.0 all-gather.2.cloned.1.call-start
  7.2 0.9 fusion.26
  8.1 0.1 broadcast_bitcast_fusion
  8.2 1.0 broadcast_multiply_fusion
  9.2 0.4 copy.12
  9.6 0.0 copy-start.1
  9.6 12.2 %all_to_all.18 = bf16[1,2,96,1024]{2,1,0,3:T(2,128)(2,1)S(1)} all-to-all(bf16[1,2,96,1024]{2,1,0,3:T(2,128)(2,1)S(1)} %copy.12), channel_id=1, replica_groups=mesh['pole'=4,'row'=4,'col'=2] {'col'}, dimensions={3} | all-to-all | bytes 786432 | tf_op jit(solution)/shard_map/all_to_all | solution.py:30
  21.8 0.8 copy.15
  22.6 0.8 copy.14
  23.4 0.0 all-gather.2.cloned.1.call-update
  23.4 0.0 copy-start
  23.4 0.0 reduce-scatter.2.cloned.1.call-start
  23.5 0.0 copy-done.1
  23.5 10.5 %all_gather.6 = bf16[1,2,4,192,192]{4,3,2,1,0:T(8,128)(2,1)S(1)} all-gather(bf16[1,2,4,96,192]{4,3,2,1,0:T(8,128)(2,1)S(1)} %copy-done.1), channel_id=1, replica_groups=mesh['pole'=4,'row'=4,'col'=2] {'col'}, dimensions={3}, use_global_device_ids=true | all-gather | bytes 884736 | tf_op jit(solution)/shard_map/all_gather | solution.py:35
  34.0 0.1 fusion.30
  34.1 0.1 bitcast_negate_fusion
  34.1 0.0 copy-done
  34.2 26.8 %all-gather.2.cloned.1.call-done = bf16[1,2,768,512]{3,2,1,0:T(8,128)(2,1)} async-done(((bf16[1,2,192,512]{3,2,1,0:T(8,128)(2,1)}), bf16[1,2,768,512]{3,2,1,0:T(8,128)(2,1)}) %all-gather.2.cloned.1.call-update) | async-done | bytes 1572880 | tf_op jit(solution)/shard_map/all_gather | solution.py:33
  61.0 1.5 slice_bitcast_fusion.1
  62.5 1.1 fusion.4
  63.6 0.0 copy-start.4
  63.6 2.1 %fusion.14 = f32[1024,512]{1,0:T(8,128)} fusion(bf16[192,512]{1,0:T(8,128)(2,1)S(1)} %get-tuple-element.10, bf16[192,512]{1,0:T(8,128)(2,1)S(1)} %fusion.29, bf16[192,512]{1,0:T(8,128)(2,1)S(1)} %get-tuple-element.9, f32[384,512]{1,0:T(8,128)S(1)} %fusion.4), kind=kOutput, calls=%fused_computation.14 | convolution fusion | flops 405995520 | bytes 3473408 | tf_op jit(solution)/shard_map/dot_general | solution.py:12
  65.7 0.0 copy-done.4
  65.7 0.0 copy-start.3
  65.7 0.0 copy-start.2
  65.7 0.0 reduce-scatter.2.cloned.1.call-update
  65.7 0.0 all-reduce.2.cloned.1.call-start
  65.8 0.6 copy-done.3
  66.3 0.6 fusion.31
  67.0 41.4 %reduce-scatter.2.cloned.1.call-done = f32[2,512,128]{2,1,0:T(8,128)} async-done(((f32[2,512,512]{2,1,0:T(8,128)}), f32[2,512,128]{2,1,0:T(8,128)}) %reduce-scatter.2.cloned.1.call-update) | async-done | bytes 524304 | tf_op jit(solution)/shard_map/reduce_scatter | solution.py:43
  108.4 0.0 copy-done.2
  108.4 1.8 %convert_bitcast_fusion = (bf16[1,2,512,128]{3,2,1,0:T(8,128)(2,1)}, f32[2,512,128]{2,1,0:T(8,128)S(1)}) fusion(f32[2,512,128]{2,1,0:T(8,128)} %reduce-scatter.2.cloned.1.call-done, bf16[1,2,512,128]{3,2,1,0:T(8,128)(2,1)S(1)} %copy-done.2), kind=kLoop, calls=%fused_computation.28 | loop fusion | flops 393216 | bytes 1572864 | tf_op jit(solution)/shard_map/broadcast_in_dim | solution.py:48
  110.2 1.9 %fusion.25 = bf16[512,128]{1,0:T(8,128)(2,1)} fusion(f32[2,512,128]{2,1,0:T(8,128)S(1)} %get-tuple-element.4, f32[]{:T(128)} %bitcast.14, f32[]{:T(128)} %bitcast.13), kind=kLoop, calls=%fused_computation.32 | loop fusion | flops 262144 | bytes 655368 | tf_op jit(solution)/shard_map/convert_element_type | solution.py:47
  112.1 0.0 all-reduce.2.cloned.1.call-update
  112.1 31.1 %all-reduce.2.cloned.1.call-done = bf16[512,128]{1,0:T(8,128)(2,1)} async-done(((bf16[512,128]{1,0:T(8,128)(2,1)}), bf16[512,128]{1,0:T(8,128)(2,1)}) %all-reduce.2.cloned.1.call-update) | async-done | bytes 131088 | tf_op jit(solution)/shard_map/psum | solution.py:47
  143.2 1.6 %convert_element_type.32 = f32[512,128]{1,0:T(8,128)} convert(bf16[512,128]{1,0:T(8,128)(2,1)} %all-reduce.2.cloned.1.call-done) | non-fusion elementwise | flops 65536 | bytes 393216 | tf_op jit(solution)/shard_map/convert_element_type | solution.py:47
  (3 shorter events, 0.1 us)
Async XLA Ops:
  7.2 53.8 %all-gather.2.cloned.1.call-start = ((), (), s32[]{:S(2)}) async-start(), calls=%async_computation.2 | async-start | bytes 1966080 | tf_op jit(solution)/shard_map/all_gather | solution.py:33
  9.6 13.9 %copy-start.1 = (bf16[1,2,4,96,192]{4,3,2,1,0:T(8,128)(2,1)S(1)}, bf16[1,2,4,96,192]{4,3,2,1,0:T(8,128)(2,1)}, u32[]{:S(2)}) copy-start(bf16[1,2,4,96,192]{4,3,2,1,0:T(8,128)(2,1)} %param.5) | copy-start | bytes 884740
  23.4 10.7 %copy-start = (bf16[1,2,2,96,512]{4,3,2,1,0:T(8,128)(2,1)S(1)}, bf16[1,2,2,96,512]{4,3,2,1,0:T(8,128)(2,1)}, u32[]{:S(2)}) copy-start(bf16[1,2,2,96,512]{4,3,2,1,0:T(8,128)(2,1)} %copy.14) | copy-start | bytes 1179652
  23.4 84.9 %reduce-scatter.2.cloned.1.call-start = ((), (), s32[]{:S(2)}) async-start(), calls=%async_computation.3 | async-start | bytes 2621440 | tf_op jit(solution)/shard_map/reduce_scatter | solution.py:43
  63.6 2.1 %copy-start.4 = (f32[384,512]{1,0:T(8,128)}, f32[384,512]{1,0:T(8,128)S(1)}, u32[]{:S(2)}) copy-start(f32[384,512]{1,0:T(8,128)S(1)} %fusion.4) | copy-start | bytes 2359300
  65.7 0.7 copy-start.3
  65.7 42.7 %copy-start.2 = (bf16[1,2,512,128]{3,2,1,0:T(8,128)(2,1)S(1)}, bf16[1,2,512,128]{3,2,1,0:T(8,128)(2,1)}, u32[]{:S(2)}) copy-start(bf16[1,2,512,128]{3,2,1,0:T(8,128)(2,1)} %param.8) | copy-start | bytes 786436
  65.7 77.5 %all-reduce.2.cloned.1.call-start = ((), (), s32[]{:S(2)}) async-start(), calls=%async_computation.4 | async-start | bytes 262144 | tf_op jit(solution)/shard_map/psum | solution.py:47
Sparse Core Ops, SparseCore 0:
  23.5 37.4 all-gather.1
  65.8 42.5 reduce-scatter.1
  112.2 30.9 all-reduce.1
where the time goes:
time: 152 us; the launch traced here: 151 us
  waiting for transfers between devices  99.4 us (65%)
  blocking collectives  22.7 us (15%)
  between operations  13.8 us (9%)
  other arithmetic  7.29 us (5%)
  local copies, waits for them, and re-layouts  4.86 us (3%)
  matrix products  3.19 us (2%)
    reduce_scatter x1, waiting for transfers between devices, body(): lax.psum_scatter(diag_terms, 'row', scatter_dimension=2, tiled=True)  41.4 us
    psum x1, waiting for transfers between devices, body(): lax.psum(density_term.astype(jnp.bfloat16), 'pole').astype(jnp.float32)  31.1 us
    all_gather x1, waiting for transfers between devices, body(): full_cols = lax.all_gather(local_rows, 'row', axis=2, tiled=True)  26.8 us
    all_to_all x1, blocking collectives, body(): lax.all_to_all(masked, 'col', split_axis=3, concat_axis=2, tiled=True)  12.2 us
    all_gather x1, blocking collectives, body(): segment = lax.all_gather(anc_inverse, 'col', axis=3, tiled=True)  10.5 us
    dot_general x2, matrix products, complex_left(): lax.dot_general(left_side, right_side, (((0,), (0,)), ((), ())), preferre...  3.19 us
  transfers between devices with their start and end apart: 3, of which 3 were waited for; matrix products, arithmetic and copies ran while one was open for 1% of the time, Pallas kernels for 0%

commit v1 on v0

v1 whole, which is shorter than its diff:
```python
import jax
import jax.numpy as jnp
from jax import lax
from jax.experimental import pallas as pl
from jax.experimental.pallas import tpu as pltpu
from jax.sharding import PartitionSpec as P


def shift(value, axis, count, step):
    return lax.ppermute(value, axis, [(i, (i + step) % count) for i in range(count)])


def named(value, axis, pairs):
    return lax.ppermute(value, axis, pairs)


VMEM = pl.BlockSpec(memory_space=pltpu.VMEM)
SMEM = pl.BlockSpec(memory_space=pltpu.SMEM)


def cut_columns(panel, pattern, n_col, width):
    def kernel(pattern_ref, panel_ref, *out_refs):
        col = lax.axis_index("col")
        row = lax.axis_index("row")
        for s in range(n_col):
            which = lax.rem(col + s, n_col)
            keep = pattern_ref[row * n_col + col, which].astype(jnp.float32)
            block = panel_ref[:, :, pl.ds(pl.multiple_of(which * width, 128), width)]
            out_refs[s][...] = (block.astype(jnp.float32) * keep).astype(jnp.bfloat16)

    shape = jax.ShapeDtypeStruct(panel.shape[:2] + (width,), jnp.bfloat16)
    return pl.pallas_call(
        kernel,
        in_specs=[SMEM, VMEM],
        out_specs=[VMEM] * n_col,
        out_shape=[shape] * n_col,
        name="cut_columns",
    )(pattern, panel)


def contract(left, right):
    return lax.dot_general(left, right, (((0,), (0,)), ((), ())), preferred_element_type=jnp.float32)


def add_products(segment_ref, q, piece_ref, sums):
    real = segment_ref[0, q]
    imag = segment_ref[1, q]
    block = piece_ref[...]
    block = block.reshape(block.shape[0] * block.shape[1], block.shape[2])
    sum_re = contract(jnp.concatenate([real, -imag], 0), block)
    sum_im = contract(jnp.concatenate([imag, real], 0), block)
    return [sum_re, sum_im] if sums is None else [sums[0] + sum_re, sums[1] + sum_im]


def early_sum(segments, pieces, n_row):
    n_col = len(segments)

    def kernel(*refs):
        row = lax.axis_index("row")
        out_ref = refs[-1]
        sums = None
        for s in range(n_col):
            for o in range(n_row):
                q = lax.rem(row + o, n_row)
                sums = add_products(refs[s], q, refs[n_col + s * n_row + o], sums)
        out_ref[0] = sums[0]
        out_ref[1] = sums[1]

    operands = list(segments) + [piece for group in pieces for piece in group]
    shape = (2, segments[0].shape[3], pieces[0][0].shape[2])
    return pl.pallas_call(
        kernel,
        in_specs=[VMEM] * len(operands),
        out_specs=VMEM,
        out_shape=jax.ShapeDtypeStruct(shape, jnp.float32),
        name="early_sum",
    )(*operands)


def late_sum(early, segments, late, n_row):
    n_late = len(late)
    rows, width = early.shape[1:]
    share = width // n_row

    def kernel(*refs):
        row = lax.axis_index("row")
        early_ref = refs[0]
        result_ref = refs[1 + n_late * 2]
        half_refs = refs[2 + n_late * 2:-1]
        rounded_ref = refs[-1]
        sums = [early_ref[0], early_ref[1]]
        q = jnp.where(row == 0, n_row - 1, 0)
        for s in range(n_late):
            sums = add_products(refs[1 + s], q, refs[1 + n_late + s], sums)
        for part in range(2):
            value = -sums[part]
            result_ref[part] = value
            rounded_ref[part] = value.astype(jnp.bfloat16)
        for o in range(n_row):
            start = pl.multiple_of(lax.rem(row + n_row - o, n_row) * share, 128)
            half_refs[o][...] = rounded_ref[:, :, pl.ds(start, share)]

    operands = [early] + (list(segments) + list(late) if late else [])
    half = jax.ShapeDtypeStruct((2, rows, share), jnp.bfloat16)
    return pl.pallas_call(
        kernel,
        in_specs=[VMEM] * len(operands),
        out_specs=[VMEM] * (1 + n_row),
        out_shape=[jax.ShapeDtypeStruct(early.shape, jnp.float32)] + [half] * n_row,
        scratch_shapes=[pltpu.VMEM(early.shape, jnp.bfloat16)],
        name="late_sum",
    )(*operands)


def diagonal(weights, diag, halves, pieces, late):
    n_row = len(halves)
    n_col = len(pieces)
    n_late = len(late)
    block_rows, width = pieces[0][0].shape[1:]
    share = halves[0].shape[2]

    def kernel(weight_ref, diag_ref, *refs):
        row = lax.axis_index("row")
        col = lax.axis_index("col")
        half_refs = refs[:n_row]
        piece_refs = refs[n_row:n_row + n_col * n_row]
        late_refs = refs[n_row + n_col * n_row:-2]
        inv_ref, sent_ref = refs[-2:]
        total = None
        for s in range(n_col):
            start = pl.multiple_of(lax.rem(col + n_col - s, n_col) * block_rows, 16)
            blocks = [ref[:, pl.ds(start, block_rows), :] for ref in half_refs]
            uses = [(blocks[o], piece_refs[s * n_row + o]) for o in range(n_row)]
            if n_late:
                uses.append((jnp.where(row == 0, blocks[n_row - 1], blocks[1]), late_refs[s]))
            for half, piece_ref in uses:
                piece = piece_ref[...].reshape(2 * block_rows, width)
                upper = jnp.concatenate([half[0], half[1]], 1)
                lower = jnp.concatenate([-half[1], half[0]], 1)
                term = contract(jnp.concatenate([upper, lower], 0), piece)
                total = term if total is None else total + term
        full_re = diag_ref[0].astype(jnp.float32) - total[:share].T
        full_im = diag_ref[1].astype(jnp.float32) - total[share:].T
        inv_ref[0] = full_re.astype(jnp.bfloat16)
        inv_ref[1] = full_im.astype(jnp.bfloat16)
        sent_ref[...] = (weight_ref[0, 0] * full_im + weight_ref[0, 1] * full_re).astype(jnp.bfloat16)

    operands = list(halves) + [piece for group in pieces for piece in group] + list(late)
    return pl.pallas_call(
        kernel,
        in_specs=[SMEM] + [VMEM] * (1 + len(operands)),
        out_specs=[VMEM, VMEM],
        out_shape=[
            jax.ShapeDtypeStruct(diag.shape, jnp.bfloat16),
            jax.ShapeDtypeStruct(diag.shape[1:], jnp.bfloat16),
        ],
        name="diagonal",
    )(weights, diag, *operands)


def body(anc_inverse, panel, pattern, diag_inverse, pole_weights):
    n_row = lax.axis_size("row")
    n_col = lax.axis_size("col")
    n_pole = lax.axis_size("pole")
    width = panel.shape[3] // n_col
    cut = cut_columns(panel[0], pattern, n_col, width)
    ring_col = lambda s: [(i, (i + s) % n_col) for i in range(n_col)]
    firsts = [cut[0]] + [named(cut[s], "col", ring_col(s)) for s in range(1, n_col)]
    segments = [anc_inverse[0]] + [named(anc_inverse[0], "col", ring_col(s)) for s in range(1, n_col)]
    pieces = []
    late = []
    for piece in firsts:
        if n_row == 4:
            far = named(piece, "row", [(0, 2), (2, 0), (1, 3), (3, 1)])
            up = named(piece, "row", [(i + 1, i) for i in range(3)])
            down = named(piece, "row", [(i, i + 1) for i in range(3)])
            late.append(named(far, "row", [(2, 3), (1, 0)]))
            pieces.append([piece, up, far, down])
        else:
            pieces.append([piece] + [shift(piece, "row", n_row, -o) for o in range(1, n_row)])
    early = early_sum(segments, pieces, n_row)
    result_panel, *blocks = late_sum(early, segments, late, n_row)
    halves = [blocks[0]]
    for o in range(1, n_row):
        halves.append(named(blocks[o], "row", [(i, (i - o) % n_row) for i in range(n_row)]))
    inv_diag, total = diagonal(pole_weights, diag_inverse[0], halves, pieces, late)
    step = 1
    while step < n_pole:
        sent = total.astype(jnp.bfloat16)
        other = lax.ppermute(sent, "pole", [(i, i ^ step) for i in range(n_pole)])
        total = sent.astype(jnp.float32) + other.astype(jnp.float32)
        step *= 2
    return result_panel[None], inv_diag[None], total


def solution(mesh):
    placed = (
        P("pole", None, None, "col", "row"),
        P("pole", None, ("row", "col"), None),
        P(),
        P("pole", None, "col", "row"),
        P("pole", None),
    )
    return jax.shard_map(
        body,
        mesh=mesh,
        in_specs=placed,
        out_specs=(P("pole", None, "row", "col"), P("pole", None, "col", "row"), P("col", "row")),
        check_vma=False,
    )
```

time: 152 us -> 73.8 us (0.49)
  waiting for transfers between devices: 99.4 us -> 24.6 us
  starting transfers between devices: 0.12 us -> 30.9 us
  blocking collectives: 22.7 us -> 0 us
  between operations: 13.8 us -> 0.84 us
  Pallas kernels: 0 us -> 11.9 us
  other arithmetic: 7.29 us -> 1.67 us
  matrix products: 3.19 us -> 0 us
    reduce_scatter x1 -> x0, waiting for transfers between devices: 41.4 us -> none  [body(): lax.psum_scatter(diag_terms, 'row', scatter_dimension=2, tiled=True)]
    psum x1 -> x0, waiting for transfers between devices: 31.1 us -> none  [body(): lax.psum(density_term.astype(jnp.bfloat16), 'pole').astype(jnp.float32)]
    ppermute x0 -> x15, starting transfers between devices: none -> 30.9 us  [the longest x13 29.4 us: named(): return lax.ppermute(value, axis, pairs)]
    all_gather x1 -> x0, waiting for transfers between devices: 26.8 us -> none  [body(): full_cols = lax.all_gather(local_rows, 'row', axis=2, tiled=True)]
    ppermute x0 -> x15, waiting for transfers between devices: none -> 24.6 us  [the longest x13 19 us: named(): return lax.ppermute(value, axis, pairs)]
    all_to_all x1 -> x0, blocking collectives: 12.2 us -> none  [body(): lax.all_to_all(masked, 'col', split_axis=3, concat_axis=2, tiled=True)]
    pallas_call x0 -> x4, Pallas kernels: none -> 11.9 us  [the longest x1 3.57 us: diagonal(): pl.pallas_call(kernel, in_specs=[SMEM] + [VMEM] * (1 + len(operands)), ou...]
    all_gather x1 -> x0, blocking collectives: 10.5 us -> none  [body(): segment = lax.all_gather(anc_inverse, 'col', axis=3, tiled=True)]
  transfers between devices with their start and end apart: 3 -> 15, of which waited for: 3 -> 7; matrix products, arithmetic and copies ran while one was open for 1% -> 0% of each run, Pallas kernels for 0% -> 5%
where the time goes in v1:
time: 73.8 us; the launch traced here: 73.4 us
  starting transfers between devices  30.9 us (42%)
  waiting for transfers between devices  24.6 us (33%)
  Pallas kernels  11.9 us (16%)
  local copies, waits for them, and re-layouts  3.44 us (5%)
  other arithmetic  1.67 us (2%)
  between operations  0.84 us (1%)
    ppermute x13, starting transfers between devices, named(): return lax.ppermute(value, axis, pairs)  29.4 us
    ppermute x13, waiting for transfers between devices, named(): return lax.ppermute(value, axis, pairs)  19 us
    ppermute x2, waiting for transfers between devices, body(): other = lax.ppermute(sent, 'pole', [(i, i ^ step) for i in range(n_pole)])  5.61 us
    pallas_call x1, Pallas kernels, diagonal(): pl.pallas_call(kernel, in_specs=[SMEM] + [VMEM] * (1 + len(operands)), ou...  3.57 us
    pallas_call x1, Pallas kernels, early_sum(): pl.pallas_call(kernel, in_specs=[VMEM] * len(operands), out_specs=VMEM, o...  3.54 us
    unnamed x29, local copies, waits for them, and re-layouts  3.44 us
    pallas_call x1, Pallas kernels, late_sum(): pl.pallas_call(kernel, in_specs=[VMEM] * len(operands), out_specs=[VMEM]...  3.01 us
    pallas_call x1, Pallas kernels, cut_columns(): pl.pallas_call(kernel, in_specs=[SMEM, VMEM], out_specs=[VMEM] * n_col, o...  1.79 us
  transfers between devices with their start and end apart: 15, of which 7 were waited for; matrix products, arithmetic and copies ran while one was open for 0% of the time, Pallas kernels for 5%

profile of v1, /device:TPU:0, one launch (start us, length us, event | category | flops | bytes accessed | tf_op | source)
XLA Modules:
  0.0 73.4 jit_solution(16222648315499026072)
XLA Ops:
  0.6 0.0 copy-start
  0.6 1.4 %copy.8.pattern_ref = s32[8,2]{1,0:T(8,128)} copy(s32[8,2]{0,1:T(2,128)} %param.7) | data formatting | bytes 128 | tf_op args[2]
  2.0 1.8 %cut_columns.1 = (bf16[2,96,512]{2,1,0:T(8,128)(2,1)}, bf16[2,96,512]{2,1,0:T(8,128)(2,1)}) custom-call(s32[8,2]{1,0:T(8,128)} %copy.8.pattern_ref, bf16[2,96,1024]{2,1,0:T(8,128)(2,1)} %bitcast.8), custom_call_target="tpu_custom_call" | custom-call | tf_op jit(solution)/shard_map/cut_columns/pallas_call | solution.py:32
  3.8 3.0 %collective-permute-start.4 = (bf16[2,96,512]{2,1,0:T(8,128)(2,1)}, bf16[2,96,512]{2,1,0:T(8,128)(2,1)S(1)}, u32[]{:S(2)}, u32[]{:S(2)}) collective-permute-start(bf16[2,96,512]{2,1,0:T(8,128)(2,1)} %get-tuple-element.13), channel_id=1, source_target_pairs={{0,1},{1,0},{2,3},{3,2},{4,5},{5,4},{6,7},{7,6},{8,9},{9,8},{10,11... | collective-permute-start | bytes 589832 | tf_op jit(solution)/shard_map/ppermute | solution.py:14
  6.8 3.5 %collective-permute-start.3 = (bf16[2,96,512]{2,1,0:T(8,128)(2,1)}, bf16[2,96,512]{2,1,0:T(8,128)(2,1)S(1)}, u32[]{:S(2)}, u32[]{:S(2)}) collective-permute-start(bf16[2,96,512]{2,1,0:T(8,128)(2,1)} %get-tuple-element.12.refs_2_.refs_4_), channel_id=1, source_target_pairs={{0,2},{2,4},{4,6},{1,3},{3,5},{5,7},{8,10},{10,12},{12,14},{9,11},... | collective-permute-start | bytes 589832 | tf_op jit(solution)/shard_map/ppermute | solution.py:14
  10.3 2.6 %collective-permute-start.2 = (bf16[2,96,512]{2,1,0:T(8,128)(2,1)}, bf16[2,96,512]{2,1,0:T(8,128)(2,1)S(1)}, u32[]{:S(2)}, u32[]{:S(2)}) collective-permute-start(bf16[2,96,512]{2,1,0:T(8,128)(2,1)} %get-tuple-element.12.refs_2_.refs_4_), channel_id=1, source_target_pairs={{0,4},{4,0},{2,6},{6,2},{1,5},{5,1},{3,7},{7,3},{8,12},{12,8},{10,... | collective-permute-start | bytes 589832 | tf_op jit(solution)/shard_map/ppermute | solution.py:14
  13.0 1.3 %collective-permute-start.1 = (bf16[2,96,512]{2,1,0:T(8,128)(2,1)}, bf16[2,96,512]{2,1,0:T(8,128)(2,1)S(1)}, u32[]{:S(2)}, u32[]{:S(2)}) collective-permute-start(bf16[2,96,512]{2,1,0:T(8,128)(2,1)} %get-tuple-element.12.refs_2_.refs_4_), channel_id=1, source_target_pairs={{2,0},{4,2},{6,4},{3,1},{5,3},{7,5},{10,8},{12,10},{14,12},{11,9},... | collective-permute-start | bytes 589832 | tf_op jit(solution)/shard_map/ppermute | solution.py:14
  14.2 0.0 collective-permute-done.4.refs_6_.refs_8_
  14.3 0.0 copy-start.2
  14.3 1.5 %collective-permute-start.6 = (bf16[2,96,512]{2,1,0:T(8,128)(2,1)S(1)}, bf16[2,96,512]{2,1,0:T(8,128)(2,1)S(1)}, u32[]{:S(2)}, u32[]{:S(2)}) collective-permute-start(bf16[2,96,512]{2,1,0:T(8,128)(2,1)S(1)} %collective-permute-done.4.refs_6_.refs_8_), channel_id=1, source_target_pairs={{0,4},{4,0},{2,6},{6,2},{1,5},{5,1},{3,7},{7,3},{8,12},{12,8},{10,... | collective-permute-start | bytes 589832 | tf_op jit(solution)/shard_map/ppermute | solution.py:14
  15.8 0.0 copy-done
  15.8 0.5 collective-permute-start
  16.3 0.0 collective-permute-done.3.refs_5_.refs_7_
  16.3 11.1 %collective-permute-start.7 = (bf16[2,96,512]{2,1,0:T(8,128)(2,1)S(1)}, bf16[2,96,512]{2,1,0:T(8,128)(2,1)S(1)}, u32[]{:S(2)}, u32[]{:S(2)}) collective-permute-start(bf16[2,96,512]{2,1,0:T(8,128)(2,1)S(1)} %collective-permute-done.4.refs_6_.refs_8_), channel_id=1, source_target_pairs={{0,2},{2,4},{4,6},{1,3},{3,5},{5,7},{8,10},{10,12},{12,14},{9,11},... | collective-permute-start | bytes 589832 | tf_op jit(solution)/shard_map/ppermute | solution.py:14
  27.4 0.0 collective-permute-done.2.refs_4_.refs_6_
  27.4 0.0 copy-start.4
  27.4 1.3 %collective-permute-start.5 = (bf16[2,96,512]{2,1,0:T(8,128)(2,1)S(1)}, bf16[2,96,512]{2,1,0:T(8,128)(2,1)S(1)}, u32[]{:S(2)}, u32[]{:S(2)}) collective-permute-start(bf16[2,96,512]{2,1,0:T(8,128)(2,1)S(1)} %collective-permute-done.4.refs_6_.refs_8_), channel_id=1, source_target_pairs={{2,0},{4,2},{6,4},{3,1},{5,3},{7,5},{10,8},{12,10},{14,12},{11,9},... | collective-permute-start | bytes 589832 | tf_op jit(solution)/shard_map/ppermute | solution.py:14
  28.7 0.0 collective-permute-done.1.refs_3_.refs_5_
  28.7 1.3 %collective-permute-start.8 = (bf16[2,96,512]{2,1,0:T(8,128)(2,1)S(1)}, bf16[2,96,512]{2,1,0:T(8,128)(2,1)S(1)}, u32[]{:S(2)}, u32[]{:S(2)}) collective-permute-start(bf16[2,96,512]{2,1,0:T(8,128)(2,1)S(1)} %collective-permute-done.2.refs_4_.refs_6_), channel_id=1, source_target_pairs={{4,6},{2,0},{5,7},{3,1},{12,14},{10,8},{13,15},{11,9},{20,22},{18,... | collective-permute-start | bytes 589832 | tf_op jit(solution)/shard_map/ppermute | solution.py:14
  30.0 5.6 %collective-permute-done.6.refs_8_.refs_10_ = bf16[2,96,512]{2,1,0:T(8,128)(2,1)S(1)} collective-permute-done((bf16[2,96,512]{2,1,0:T(8,128)(2,1)S(1)}, bf16[2,96,512]{2,1,0:T(8,128)(2,1)S(1)}, u32[]{:S(2)}, u32[]{:S(2)}) %collective-permute-start.6) | collective-permute-done | bytes 196640 | tf_op jit(solution)/shard_map/ppermute | solution.py:14
  35.6 1.3 %collective-permute-start.9 = (bf16[2,96,512]{2,1,0:T(8,128)(2,1)S(1)}, bf16[2,96,512]{2,1,0:T(8,128)(2,1)S(1)}, u32[]{:S(2)}, u32[]{:S(2)}) collective-permute-start(bf16[2,96,512]{2,1,0:T(8,128)(2,1)S(1)} %collective-permute-done.6.refs_8_.refs_10_), channel_id=1, source_target_pairs={{4,6},{2,0},{5,7},{3,1},{12,14},{10,8},{13,15},{11,9},{20,22},{18,... | collective-permute-start | bytes 589832 | tf_op jit(solution)/shard_map/ppermute | solution.py:14
  36.9 0.0 collective-permute-done.refs_1_.refs_2_
  36.9 0.0 collective-permute-done.7.refs_9_.refs_11_
  36.9 0.0 copy-start.7
  36.9 1.9 %collective-permute-done.5.refs_7_.refs_9_ = bf16[2,96,512]{2,1,0:T(8,128)(2,1)S(1)} collective-permute-done((bf16[2,96,512]{2,1,0:T(8,128)(2,1)S(1)}, bf16[2,96,512]{2,1,0:T(8,128)(2,1)S(1)}, u32[]{:S(2)}, u32[]{:S(2)}) %collective-permute-start.5) | collective-permute-done | bytes 196640 | tf_op jit(solution)/shard_map/ppermute | solution.py:14
  38.8 0.0 copy-done.4
  38.9 0.7 copy-done.8
  39.5 3.5 %early_sum.1.refs_0_ = f32[2,192,512]{2,1,0:T(8,128)} custom-call(bf16[2,4,96,192]{3,2,1,0:T(8,128)(2,1)} %bitcast.5, bf16[2,4,96,192]{3,2,1,0:T(8,128)(2,1)} %copy-done.1, bf16[2,96,512]{2,1,0:T(8,128)(2,1)} %get-tuple-element.12.refs_2_.refs_4_, bf16[2,96,512]{2,1,0:T(8,128)(2,1)} %copy-done.5, bf16[2,96,512]{2,1,0:T(8,128)(2,1)} %copy-done.4, ...), custom_call_target="tpu_custom_call" | custom-call | tf_op jit(solution)/shard_map/early_sum/pallas_call | solution.py:71
  43.1 0.0 collective-permute-done.8.refs_3_.refs_12_
  43.1 3.4 %collective-permute-done.9.refs_4_.refs_13_ = bf16[2,96,512]{2,1,0:T(8,128)(2,1)S(1)} collective-permute-done((bf16[2,96,512]{2,1,0:T(8,128)(2,1)S(1)}, bf16[2,96,512]{2,1,0:T(8,128)(2,1)S(1)}, u32[]{:S(2)}, u32[]{:S(2)}) %collective-permute-start.9) | collective-permute-done | bytes 196640 | tf_op jit(solution)/shard_map/ppermute | solution.py:14
  46.5 0.0 copy-done.9
  46.5 0.7 copy-done.10
  47.1 3.0 %late_sum.1 = (f32[2,192,512]{2,1,0:T(8,128)}, bf16[2,192,128]{2,1,0:T(8,128)(2,1)}, bf16[2,192,128]{2,1,0:T(8,128)(2,1)}, bf16[2,192,128]{2,1,0:T(8,128)(2,1)}, bf16[2,192,128]{2,1,0:T(8,128)(2,1)}) custom-call(f32[2,192,512]{2,1,0:T(8,128)} %early_sum.1.refs_0_, bf16[2,4,96,192]{3,2,1,0:T(8,128)(2,1)} %bitcast.6, bf16[2,4,96,192]{3,2,1,0:T(8,128)(2,1)} %copy-done.1, ...), custom_call_target="tpu_custom_call" | custom-call | tf_op jit(solution)/shard_map/late_sum/pallas_call | solution.py:105
  50.2 0.0 collective-permute-start.10
  50.2 1.0 %collective-permute-start.11 = (bf16[2,192,128]{2,1,0:T(8,128)(2,1)}, bf16[2,192,128]{2,1,0:T(8,128)(2,1)S(1)}, u32[]{:S(2)}, u32[]{:S(2)}) collective-permute-start(bf16[2,192,128]{2,1,0:T(8,128)(2,1)} %get-tuple-element.17), channel_id=1, source_target_pairs={{0,4},{2,6},{4,0},{6,2},{1,5},{3,7},{5,1},{7,3},{8,12},{10,14},{12... | collective-permute-start | bytes 294920 | tf_op jit(solution)/shard_map/ppermute | solution.py:14
  51.2 1.0 %collective-permute-start.12 = (bf16[2,192,128]{2,1,0:T(8,128)(2,1)}, bf16[2,192,128]{2,1,0:T(8,128)(2,1)S(1)}, u32[]{:S(2)}, u32[]{:S(2)}) collective-permute-start(bf16[2,192,128]{2,1,0:T(8,128)(2,1)} %get-tuple-element.18), channel_id=1, source_target_pairs={{0,2},{2,4},{4,6},{6,0},{1,3},{3,5},{5,7},{7,1},{8,10},{10,12},{12... | collective-permute-start | bytes 294920 | tf_op jit(solution)/shard_map/ppermute | solution.py:14
  52.2 3.1 %collective-permute-done.10.refs_1_ = bf16[2,192,128]{2,1,0:T(8,128)(2,1)S(1)} collective-permute-done((bf16[2,192,128]{2,1,0:T(8,128)(2,1)}, bf16[2,192,128]{2,1,0:T(8,128)(2,1)S(1)}, u32[]{:S(2)}, u32[]{:S(2)}) %collective-permute-start.10) | collective-permute-done | bytes 98336 | tf_op jit(solution)/shard_map/ppermute | solution.py:14
  55.3 5.0 %collective-permute-done.11.refs_2_ = bf16[2,192,128]{2,1,0:T(8,128)(2,1)S(1)} collective-permute-done((bf16[2,192,128]{2,1,0:T(8,128)(2,1)}, bf16[2,192,128]{2,1,0:T(8,128)(2,1)S(1)}, u32[]{:S(2)}, u32[]{:S(2)}) %collective-permute-start.11) | collective-permute-done | bytes 98336 | tf_op jit(solution)/shard_map/ppermute | solution.py:14
  60.3 0.0 collective-permute-done.12.refs_3_
  60.3 0.6 copy-done.12
  60.9 0.0 copy-done.13
  61.0 3.6 %diagonal.1 = (bf16[2,512,128]{2,1,0:T(8,128)(2,1)}, bf16[512,128]{1,0:T(8,128)(2,1)}) custom-call(f32[1,2]{1,0:T(1,128)} %weight_ref.1, bf16[2,512,128]{2,1,0:T(8,128)(2,1)} %bitcast.9, bf16[2,192,128]{2,1,0:T(8,128)(2,1)} %get-tuple-element.15.refs_0_, bf16[2,192,128]{2,1,0:T(8,128)(2,1)} %copy-done.11, bf16[2,192,128]{2,1,0:T(8,128)(2,1)} %copy-done.12, ...), custom_call_target="tpu_custom_call" | custom-call | tf_op jit(solution)/shard_map/diagonal/pallas_call | solution.py:149
  64.5 0.0 collective-permute-start.13
  64.5 1.6 %collective-permute-done.13 = bf16[512,128]{1,0:T(8,128)(2,1)S(1)} collective-permute-done((bf16[512,128]{1,0:T(8,128)(2,1)}, bf16[512,128]{1,0:T(8,128)(2,1)S(1)}, u32[]{:S(2)}, u32[]{:S(2)}) %collective-permute-start.13) | collective-permute-done | bytes 131104 | tf_op jit(solution)/shard_map/ppermute | solution.py:190
  66.1 0.9 %add_convert_fusion = bf16[512,128]{1,0:T(8,128)(2,1)S(1)} fusion(bf16[512,128]{1,0:T(8,128)(2,1)S(1)} %collective-permute-done.13, bf16[512,128]{1,0:T(8,128)(2,1)} %get-tuple-element.20), kind=kLoop, calls=%fused_computation.1 | loop fusion | flops 262144 | bytes 393216 | tf_op jit(solution)/shard_map/convert_element_type | solution.py:189
  67.0 1.6 %collective-permute-start.14 = (bf16[512,128]{1,0:T(8,128)(2,1)S(1)}, bf16[512,128]{1,0:T(8,128)(2,1)S(1)}, u32[]{:S(2)}, u32[]{:S(2)}) collective-permute-start(bf16[512,128]{1,0:T(8,128)(2,1)S(1)} %add_convert_fusion), channel_id=1, source_target_pairs={{0,16},{8,24},{16,0},{24,8},{1,17},{9,25},{17,1},{25,9},{2,18},{10... | collective-permute-start | bytes 393224 | tf_op jit(solution)/shard_map/ppermute | solution.py:190
  68.6 4.1 %collective-permute-done.14 = bf16[512,128]{1,0:T(8,128)(2,1)S(1)} collective-permute-done((bf16[512,128]{1,0:T(8,128)(2,1)S(1)}, bf16[512,128]{1,0:T(8,128)(2,1)S(1)}, u32[]{:S(2)}, u32[]{:S(2)}) %collective-permute-start.14) | collective-permute-done | bytes 131104 | tf_op jit(solution)/shard_map/ppermute | solution.py:190
  72.7 0.7 convert_add_fusion
  (17 shorter events, 0.0 us)
Async XLA Ops:
  0.6 15.2 %copy-start = (bf16[1,2,4,96,192]{4,3,2,1,0:T(8,128)(2,1)S(1)}, bf16[1,2,4,96,192]{4,3,2,1,0:T(8,128)(2,1)}, u32[]{:S(2)}) copy-start(bf16[1,2,4,96,192]{4,3,2,1,0:T(8,128)(2,1)} %param.5) | copy-start | bytes 884740
  3.8 10.4 %collective-permute-start.4 = (bf16[2,96,512]{2,1,0:T(8,128)(2,1)}, bf16[2,96,512]{2,1,0:T(8,128)(2,1)S(1)}, u32[]{:S(2)}, u32[]{:S(2)}) collective-permute-start(bf16[2,96,512]{2,1,0:T(8,128)(2,1)} %get-tuple-element.13), channel_id=1, source_target_pairs={{0,1},{1,0},{2,3},{3,2},{4,5},{5,4},{6,7},{7,6},{8,9},{9,8},{10,11... | collective-permute-start | bytes 589832 | tf_op jit(solution)/shard_map/ppermute | solution.py:14
  6.8 9.5 %collective-permute-start.3 = (bf16[2,96,512]{2,1,0:T(8,128)(2,1)}, bf16[2,96,512]{2,1,0:T(8,128)(2,1)S(1)}, u32[]{:S(2)}, u32[]{:S(2)}) collective-permute-start(bf16[2,96,512]{2,1,0:T(8,128)(2,1)} %get-tuple-element.12.refs_2_.refs_4_), channel_id=1, source_target_pairs={{0,2},{2,4},{4,6},{1,3},{3,5},{5,7},{8,10},{10,12},{12,14},{9,11},... | collective-permute-start | bytes 589832 | tf_op jit(solution)/shard_map/ppermute | solution.py:14
  10.3 17.1 %collective-permute-start.2 = (bf16[2,96,512]{2,1,0:T(8,128)(2,1)}, bf16[2,96,512]{2,1,0:T(8,128)(2,1)S(1)}, u32[]{:S(2)}, u32[]{:S(2)}) collective-permute-start(bf16[2,96,512]{2,1,0:T(8,128)(2,1)} %get-tuple-element.12.refs_2_.refs_4_), channel_id=1, source_target_pairs={{0,4},{4,0},{2,6},{6,2},{1,5},{5,1},{3,7},{7,3},{8,12},{12,8},{10,... | collective-permute-start | bytes 589832 | tf_op jit(solution)/shard_map/ppermute | solution.py:14
  13.0 15.7 %collective-permute-start.1 = (bf16[2,96,512]{2,1,0:T(8,128)(2,1)}, bf16[2,96,512]{2,1,0:T(8,128)(2,1)S(1)}, u32[]{:S(2)}, u32[]{:S(2)}) collective-permute-start(bf16[2,96,512]{2,1,0:T(8,128)(2,1)} %get-tuple-element.12.refs_2_.refs_4_), channel_id=1, source_target_pairs={{2,0},{4,2},{6,4},{3,1},{5,3},{7,5},{10,8},{12,10},{14,12},{11,9},... | collective-permute-start | bytes 589832 | tf_op jit(solution)/shard_map/ppermute | solution.py:14
  14.3 24.6 %copy-start.2 = (bf16[2,96,512]{2,1,0:T(8,128)(2,1)}, bf16[2,96,512]{2,1,0:T(8,128)(2,1)S(1)}, u32[]{:S(2)}) copy-start(bf16[2,96,512]{2,1,0:T(8,128)(2,1)S(1)} %collective-permute-done.4.refs_6_.refs_8_) | copy-start | bytes 589828
  14.3 21.3 %collective-permute-start.6 = (bf16[2,96,512]{2,1,0:T(8,128)(2,1)S(1)}, bf16[2,96,512]{2,1,0:T(8,128)(2,1)S(1)}, u32[]{:S(2)}, u32[]{:S(2)}) collective-permute-start(bf16[2,96,512]{2,1,0:T(8,128)(2,1)S(1)} %collective-permute-done.4.refs_6_.refs_8_), channel_id=1, source_target_pairs={{0,4},{4,0},{2,6},{6,2},{1,5},{5,1},{3,7},{7,3},{8,12},{12,8},{10,... | collective-permute-start | bytes 589832 | tf_op jit(solution)/shard_map/ppermute | solution.py:14
  15.8 21.1 %collective-permute-start = (bf16[2,4,96,192]{3,2,1,0:T(8,128)(2,1)S(1)}, bf16[2,4,96,192]{3,2,1,0:T(8,128)(2,1)S(1)}, u32[]{:S(2)}, u32[]{:S(2)}) collective-permute-start(bf16[2,4,96,192]{3,2,1,0:T(8,128)(2,1)S(1)} %bitcast.7), channel_id=1, source_target_pairs={{0,1},{1,0},{2,3},{3,2},{4,5},{5,4},{6,7},{7,6},{8,9},{9,8},{10,11... | collective-permute-start | bytes 884744 | tf_op jit(solution)/shard_map/ppermute | solution.py:14
  16.3 22.5 %copy-start.3 = (bf16[2,96,512]{2,1,0:T(8,128)(2,1)}, bf16[2,96,512]{2,1,0:T(8,128)(2,1)S(1)}, u32[]{:S(2)}) copy-start(bf16[2,96,512]{2,1,0:T(8,128)(2,1)S(1)} %collective-permute-done.3.refs_5_.refs_7_) | copy-start | bytes 589828
  16.3 20.6 %collective-permute-start.7 = (bf16[2,96,512]{2,1,0:T(8,128)(2,1)S(1)}, bf16[2,96,512]{2,1,0:T(8,128)(2,1)S(1)}, u32[]{:S(2)}, u32[]{:S(2)}) collective-permute-start(bf16[2,96,512]{2,1,0:T(8,128)(2,1)S(1)} %collective-permute-done.4.refs_6_.refs_8_), channel_id=1, source_target_pairs={{0,2},{2,4},{4,6},{1,3},{3,5},{5,7},{8,10},{10,12},{12,14},{9,11},... | collective-permute-start | bytes 589832 | tf_op jit(solution)/shard_map/ppermute | solution.py:14
  27.4 11.4 %copy-start.4 = (bf16[2,96,512]{2,1,0:T(8,128)(2,1)}, bf16[2,96,512]{2,1,0:T(8,128)(2,1)S(1)}, u32[]{:S(2)}) copy-start(bf16[2,96,512]{2,1,0:T(8,128)(2,1)S(1)} %collective-permute-done.2.refs_4_.refs_6_) | copy-start | bytes 589828
  27.4 11.4 %collective-permute-start.5 = (bf16[2,96,512]{2,1,0:T(8,128)(2,1)S(1)}, bf16[2,96,512]{2,1,0:T(8,128)(2,1)S(1)}, u32[]{:S(2)}, u32[]{:S(2)}) collective-permute-start(bf16[2,96,512]{2,1,0:T(8,128)(2,1)S(1)} %collective-permute-done.4.refs_6_.refs_8_), channel_id=1, source_target_pairs={{2,0},{4,2},{6,4},{3,1},{5,3},{7,5},{10,8},{12,10},{14,12},{11,9},... | collective-permute-start | bytes 589832 | tf_op jit(solution)/shard_map/ppermute | solution.py:14
  28.7 10.1 %copy-start.5 = (bf16[2,96,512]{2,1,0:T(8,128)(2,1)}, bf16[2,96,512]{2,1,0:T(8,128)(2,1)S(1)}, u32[]{:S(2)}) copy-start(bf16[2,96,512]{2,1,0:T(8,128)(2,1)S(1)} %collective-permute-done.1.refs_3_.refs_5_) | copy-start | bytes 589828
  28.7 14.4 %collective-permute-start.8 = (bf16[2,96,512]{2,1,0:T(8,128)(2,1)S(1)}, bf16[2,96,512]{2,1,0:T(8,128)(2,1)S(1)}, u32[]{:S(2)}, u32[]{:S(2)}) collective-permute-start(bf16[2,96,512]{2,1,0:T(8,128)(2,1)S(1)} %collective-permute-done.2.refs_4_.refs_6_), channel_id=1, source_target_pairs={{4,6},{2,0},{5,7},{3,1},{12,14},{10,8},{13,15},{11,9},{20,22},{18,... | collective-permute-start | bytes 589832 | tf_op jit(solution)/shard_map/ppermute | solution.py:14
  35.6 3.3 %copy-start.6 = (bf16[2,96,512]{2,1,0:T(8,128)(2,1)}, bf16[2,96,512]{2,1,0:T(8,128)(2,1)S(1)}, u32[]{:S(2)}) copy-start(bf16[2,96,512]{2,1,0:T(8,128)(2,1)S(1)} %collective-permute-done.6.refs_8_.refs_10_) | copy-start | bytes 589828
  35.6 10.9 %collective-permute-start.9 = (bf16[2,96,512]{2,1,0:T(8,128)(2,1)S(1)}, bf16[2,96,512]{2,1,0:T(8,128)(2,1)S(1)}, u32[]{:S(2)}, u32[]{:S(2)}) collective-permute-start(bf16[2,96,512]{2,1,0:T(8,128)(2,1)S(1)} %collective-permute-done.6.refs_8_.refs_10_), channel_id=1, source_target_pairs={{4,6},{2,0},{5,7},{3,1},{12,14},{10,8},{13,15},{11,9},{20,22},{18,... | collective-permute-start | bytes 589832 | tf_op jit(solution)/shard_map/ppermute | solution.py:14
  36.9 2.0 %copy-start.1 = (bf16[2,4,96,192]{3,2,1,0:T(8,128)(2,1)}, bf16[2,4,96,192]{3,2,1,0:T(8,128)(2,1)S(1)}, u32[]{:S(2)}) copy-start(bf16[2,4,96,192]{3,2,1,0:T(8,128)(2,1)S(1)} %collective-permute-done.refs_1_.refs_2_) | copy-start | bytes 884740
  36.9 2.0 %copy-start.7 = (bf16[2,96,512]{2,1,0:T(8,128)(2,1)}, bf16[2,96,512]{2,1,0:T(8,128)(2,1)S(1)}, u32[]{:S(2)}) copy-start(bf16[2,96,512]{2,1,0:T(8,128)(2,1)S(1)} %collective-permute-done.7.refs_9_.refs_11_) | copy-start | bytes 589828
  38.9 0.7 copy-start.8
  43.1 3.4 %copy-start.9 = (bf16[2,96,512]{2,1,0:T(8,128)(2,1)}, bf16[2,96,512]{2,1,0:T(8,128)(2,1)S(1)}, u32[]{:S(2)}) copy-start(bf16[2,96,512]{2,1,0:T(8,128)(2,1)S(1)} %collective-permute-done.8.refs_3_.refs_12_) | copy-start | bytes 589828
  46.5 0.7 copy-start.10
  50.2 5.1 %collective-permute-start.10 = (bf16[2,192,128]{2,1,0:T(8,128)(2,1)}, bf16[2,192,128]{2,1,0:T(8,128)(2,1)S(1)}, u32[]{:S(2)}, u32[]{:S(2)}) collective-permute-start(bf16[2,192,128]{2,1,0:T(8,128)(2,1)} %get-tuple-element.16), channel_id=1, source_target_pairs={{0,6},{2,0},{4,2},{6,4},{1,7},{3,1},{5,3},{7,5},{8,14},{10,8},{12,... | collective-permute-start | bytes 294920 | tf_op jit(solution)/shard_map/ppermute | solution.py:14
  50.2 10.1 %collective-permute-start.11 = (bf16[2,192,128]{2,1,0:T(8,128)(2,1)}, bf16[2,192,128]{2,1,0:T(8,128)(2,1)S(1)}, u32[]{:S(2)}, u32[]{:S(2)}) collective-permute-start(bf16[2,192,128]{2,1,0:T(8,128)(2,1)} %get-tuple-element.17), channel_id=1, source_target_pairs={{0,4},{2,6},{4,0},{6,2},{1,5},{3,7},{5,1},{7,3},{8,12},{10,14},{12... | collective-permute-start | bytes 294920 | tf_op jit(solution)/shard_map/ppermute | solution.py:14
  51.2 9.1 %collective-permute-start.12 = (bf16[2,192,128]{2,1,0:T(8,128)(2,1)}, bf16[2,192,128]{2,1,0:T(8,128)(2,1)S(1)}, u32[]{:S(2)}, u32[]{:S(2)}) collective-permute-start(bf16[2,192,128]{2,1,0:T(8,128)(2,1)} %get-tuple-element.18), channel_id=1, source_target_pairs={{0,2},{2,4},{4,6},{6,0},{1,3},{3,5},{5,7},{7,1},{8,10},{10,12},{12... | collective-permute-start | bytes 294920 | tf_op jit(solution)/shard_map/ppermute | solution.py:14
  55.3 5.0 %copy-start.11 = (bf16[2,192,128]{2,1,0:T(8,128)(2,1)}, bf16[2,192,128]{2,1,0:T(8,128)(2,1)S(1)}, u32[]{:S(2)}) copy-start(bf16[2,192,128]{2,1,0:T(8,128)(2,1)S(1)} %collective-permute-done.10.refs_1_) | copy-start | bytes 294916
  60.3 0.6 copy-start.12
  60.3 0.7 copy-start.13
  64.5 1.6 %collective-permute-start.13 = (bf16[512,128]{1,0:T(8,128)(2,1)}, bf16[512,128]{1,0:T(8,128)(2,1)S(1)}, u32[]{:S(2)}, u32[]{:S(2)}) collective-permute-start(bf16[512,128]{1,0:T(8,128)(2,1)} %get-tuple-element.20), channel_id=1, source_target_pairs={{0,8},{8,0},{16,24},{24,16},{1,9},{9,1},{17,25},{25,17},{2,10},{10... | collective-permute-start | bytes 393224 | tf_op jit(solution)/shard_map/ppermute | solution.py:190
  67.0 5.6 %collective-permute-start.14 = (bf16[512,128]{1,0:T(8,128)(2,1)S(1)}, bf16[512,128]{1,0:T(8,128)(2,1)S(1)}, u32[]{:S(2)}, u32[]{:S(2)}) collective-permute-start(bf16[512,128]{1,0:T(8,128)(2,1)S(1)} %add_convert_fusion), channel_id=1, source_target_pairs={{0,16},{8,24},{16,0},{24,8},{1,17},{9,25},{17,1},{25,9},{2,18},{10... | collective-permute-start | bytes 393224 | tf_op jit(solution)/shard_map/ppermute | solution.py:190

commit v2 on v1

v2 whole, which is shorter than its diff:
```python
import jax
import jax.numpy as jnp
from jax import lax
from jax.experimental import pallas as pl
from jax.experimental.pallas import tpu as pltpu
from jax.sharding import PartitionSpec as P


def shift(value, axis, count, step):
    return lax.ppermute(value, axis, [(i, (i + step) % count) for i in range(count)])


VMEM = pl.BlockSpec(memory_space=pltpu.VMEM)
SMEM = pl.BlockSpec(memory_space=pltpu.SMEM)


def in_vmem(operands, near):
    if not near:
        return list(operands)
    return [pltpu.with_memory_space_constraint(operand, pltpu.VMEM) for operand in operands]


def result_of(near, shape, dtype):
    return pltpu.VMEM(shape, dtype) if near else jax.ShapeDtypeStruct(shape, dtype)


def cut_columns(panel, n_col, width, near):
    def kernel(panel_ref, *out_refs):
        col = lax.axis_index("col")
        for s in range(n_col):
            which = lax.rem(col + s, n_col)
            out_refs[s][...] = panel_ref[:, :, pl.ds(pl.multiple_of(which * width, 128), width)]

    return pl.pallas_call(
        kernel,
        in_specs=[VMEM],
        out_specs=[VMEM] * n_col,
        out_shape=[result_of(near, panel.shape[:2] + (width,), jnp.bfloat16)] * n_col,
        name="cut_columns",
    )(panel)


def kept(block, pattern_ref, q, s, n_col):
    col = lax.axis_index("col")
    keep = pattern_ref[q * n_col + lax.rem(col + n_col - s, n_col), col]
    return (block.astype(jnp.float32) * keep.astype(jnp.float32)).astype(jnp.bfloat16)


def contract(left, right):
    return lax.dot_general(left, right, (((0,), (0,)), ((), ())), preferred_element_type=jnp.float32)


def add_products(pattern_ref, segment_ref, q, s, n_col, piece_ref, sums):
    real = kept(segment_ref[0, q], pattern_ref, q, s, n_col)
    imag = kept(segment_ref[1, q], pattern_ref, q, s, n_col)
    block = piece_ref[...]
    block = block.reshape(block.shape[0] * block.shape[1], block.shape[2])
    sum_re = contract(jnp.concatenate([real, -imag], 0), block)
    sum_im = contract(jnp.concatenate([imag, real], 0), block)
    return [sum_re, sum_im] if sums is None else [sums[0] + sum_re, sums[1] + sum_im]


def early_sum(pattern, segments, pieces, n_row, near):
    n_col = len(segments)

    def kernel(pattern_ref, *refs):
        row = lax.axis_index("row")
        out_ref = refs[-1]
        sums = None
        for s in range(n_col):
            for o in range(n_row):
                q = lax.rem(row + o, n_row)
                sums = add_products(pattern_ref, refs[s], q, s, n_col, refs[n_col + s * n_row + o], sums)
        out_ref[0] = sums[0]
        out_ref[1] = sums[1]

    operands = list(segments) + in_vmem([piece for group in pieces for piece in group], near)
    shape = (2, segments[0].shape[3], pieces[0][0].shape[2])
    return pl.pallas_call(
        kernel,
        in_specs=[SMEM] + [VMEM] * len(operands),
        out_specs=VMEM,
        out_shape=result_of(near, shape, jnp.float32),
        name="early_sum",
    )(pattern, *operands)


def late_sum(pattern, early, segments, late, n_row, whole, near):
    n_col = len(segments)
    n_late = len(late)
    rows, width = early.shape[1:]
    share = width // n_row

    def kernel(pattern_ref, early_ref, *refs):
        row = lax.axis_index("row")
        outs = refs[2 * n_late:]
        sums = [early_ref[0], early_ref[1]]
        q = jnp.where(row == 0, n_row - 1, 0)
        for s in range(n_late):
            sums = add_products(pattern_ref, refs[s], q, s, n_col, refs[n_late + s], sums)
        if whole:
            outs[0][0] = -sums[0]
            outs[0][1] = -sums[1]
            return
        rounded_ref = outs[-1]
        rounded_ref[0] = (-sums[0]).astype(jnp.bfloat16)
        rounded_ref[1] = (-sums[1]).astype(jnp.bfloat16)
        for o in range(n_row):
            start = pl.multiple_of(lax.rem(row + n_row - o, n_row) * share, 128)
            outs[o][...] = rounded_ref[:, :, pl.ds(start, share)]

    operands = in_vmem([early], near) + (list(segments) + in_vmem(late, near) if late else [])
    half = result_of(near, (2, rows, share), jnp.bfloat16)
    return pl.pallas_call(
        kernel,
        in_specs=[SMEM] + [VMEM] * len(operands),
        out_specs=[VMEM] * (1 if whole else n_row),
        out_shape=[jax.ShapeDtypeStruct(early.shape, jnp.float32)] if whole else [half] * n_row,
        scratch_shapes=[] if whole else [pltpu.VMEM(early.shape, jnp.bfloat16)],
        name="whole_sum" if whole else "late_sum",
    )(pattern, *operands)


def diagonal(weights, pattern, diag, halves, pieces, late, near):
    n_row = len(halves)
    n_col = len(pieces)
    n_late = len(late)
    block_rows, width = pieces[0][0].shape[1:]
    share = halves[0].shape[2]

    def kernel(weight_ref, pattern_ref, diag_ref, *refs):
        row = lax.axis_index("row")
        col = lax.axis_index("col")
        half_refs = refs[:n_row]
        piece_refs = refs[n_row:n_row + n_col * n_row]
        late_refs = refs[n_row + n_col * n_row:-2]
        inv_ref, sent_ref = refs[-2:]
        total = None
        for s in range(n_col):
            start = pl.multiple_of(lax.rem(col + n_col - s, n_col) * block_rows, 16)
            blocks = [ref[:, pl.ds(start, block_rows), :] for ref in half_refs]
            uses = [(blocks[o], lax.rem(row + o, n_row), piece_refs[s * n_row + o]) for o in range(n_row)]
            if n_late:
                other = jnp.where(row == 0, blocks[n_row - 1], blocks[1])
                uses.append((other, jnp.where(row == 0, n_row - 1, 0), late_refs[s]))
            for half, q, piece_ref in uses:
                half = kept(half, pattern_ref, q, s, n_col)
                piece = piece_ref[...].reshape(2 * block_rows, width)
                upper = jnp.concatenate([half[0], half[1]], 1)
                lower = jnp.concatenate([-half[1], half[0]], 1)
                term = contract(jnp.concatenate([upper, lower], 0), piece)
                total = term if total is None else total + term
        full_re = diag_ref[0].astype(jnp.float32) - total[:share].T
        full_im = diag_ref[1].astype(jnp.float32) - total[share:].T
        inv_ref[0] = full_re.astype(jnp.bfloat16)
        inv_ref[1] = full_im.astype(jnp.bfloat16)
        sent_ref[...] = (weight_ref[0, 0] * full_im + weight_ref[0, 1] * full_re).astype(jnp.bfloat16)

    operands = in_vmem(list(halves) + [piece for group in pieces for piece in group] + list(late), near)
    return pl.pallas_call(
        kernel,
        in_specs=[SMEM, SMEM] + [VMEM] * (1 + len(operands)),
        out_specs=[VMEM, VMEM],
        out_shape=[
            jax.ShapeDtypeStruct(diag.shape, jnp.bfloat16),
            result_of(near, diag.shape[1:], jnp.bfloat16),
        ],
        name="diagonal",
    )(weights, pattern, diag, *operands)


def body(anc_inverse, panel, pattern, diag_inverse, pole_weights):
    n_row = lax.axis_size("row")
    n_col = lax.axis_size("col")
    n_pole = lax.axis_size("pole")
    width = panel.shape[3] // n_col
    held = 2 * width * (2 * panel.shape[2] * n_col * (n_row + 1) + 4 * anc_inverse.shape[4])
    near = held <= 3 * 2**20
    cut = cut_columns(panel[0], n_col, width, near)
    ring_col = lambda s: [(i, (i + s) % n_col) for i in range(n_col)]
    firsts = [cut[0]] + [lax.ppermute(cut[s], "col", ring_col(s)) for s in range(1, n_col)]
    segments = [anc_inverse[0]] + [lax.ppermute(anc_inverse[0], "col", ring_col(s)) for s in range(1, n_col)]
    pieces = []
    late = []
    for piece in firsts:
        if n_row == 4:
            far = lax.ppermute(piece, "row", [(0, 2), (2, 0), (1, 3), (3, 1)])
            up = lax.ppermute(piece, "row", [(i + 1, i) for i in range(3)])
            down = lax.ppermute(piece, "row", [(i, i + 1) for i in range(3)])
            late.append(lax.ppermute(far, "row", [(2, 3), (1, 0)]))
            pieces.append([piece, up, far, down])
        else:
            pieces.append([piece] + [shift(piece, "row", n_row, -o) for o in range(1, n_row)])
    early = early_sum(pattern, segments, pieces, n_row, near)
    blocks = late_sum(pattern, early, segments, late, n_row, False, near)
    (result_panel,) = late_sum(pattern, early, segments, late, n_row, True, near)
    halves = [blocks[0]]
    for o in range(1, n_row):
        halves.append(lax.ppermute(blocks[o], "row", [(i, (i - o) % n_row) for i in range(n_row)]))
    inv_diag, total = diagonal(pole_weights, pattern, diag_inverse[0], halves, pieces, late, near)
    step = 1
    while step < n_pole:
        sent = total.astype(jnp.bfloat16)
        other = lax.ppermute(sent, "pole", [(i, i ^ step) for i in range(n_pole)])
        total = sent.astype(jnp.float32) + other.astype(jnp.float32)
        step *= 2
    return result_panel[None], inv_diag[None], total


def solution(mesh):
    placed = (
        P("pole", None, None, "col", "row"),
        P("pole", None, ("row", "col"), None),
        P(),
        P("pole", None, "col", "row"),
        P("pole", None),
    )
    return jax.shard_map(
        body,
        mesh=mesh,
        in_specs=placed,
        out_specs=(P("pole", None, "row", "col"), P("pole", None, "col", "row"), P("col", "row")),
        check_vma=False,
    )
```

time: 73.8 us -> 65.7 us (0.89)
  waiting for transfers between devices: 24.6 us -> 17.8 us
  starting transfers between devices: 30.9 us -> 33.4 us
  Pallas kernels: 11.9 us -> 10.2 us
  local copies, waits for them, and re-layouts: 3.44 us -> 2.36 us
  other arithmetic: 1.67 us -> 0.77 us
    ppermute x13, waiting for transfers between devices: 19 us -> 14.8 us  [the longest x3 7.26 us: body(): lax.ppermute(blocks[o], 'row', [(i, (i - o) % n_row) for i in range(n_row)])]
    ppermute x2, waiting for transfers between devices: 5.61 us -> 2.99 us  [body(): other = lax.ppermute(sent, 'pole', [(i, i ^ step) for i in range(n_pole)])]
    ppermute x13, starting transfers between devices: 29.4 us -> 31.9 us  [the longest x2 13.3 us: body(): down = lax.ppermute(piece, 'row', [(i, i + 1) for i in range(3)])]
    pallas_call x4 -> x5, Pallas kernels: 11.9 us -> 10.2 us  [the longest x2 4.08 us: late_sum(): pl.pallas_call(kernel, in_specs=[SMEM] + [VMEM] * len(operands), out_spec...]
    unnamed x29 -> x15, local copies, waits for them, and re-layouts: 3.44 us -> 2.36 us
    convert_element_type x1, other arithmetic: 0.94 us -> 0.04 us  [body(): sent = total.astype(jnp.bfloat16)]
  transfers between devices with their start and end apart: 15 -> 15, of which waited for: 7 -> 8; matrix products, arithmetic and copies ran while one was open for 0% -> 1% of each run, Pallas kernels for 5% -> 7%
where the time goes in v2:
time: 65.7 us; the launch traced here: 65.3 us
  starting transfers between devices  33.4 us (51%)
  waiting for transfers between devices  17.8 us (27%)
  Pallas kernels  10.2 us (16%)
  local copies, waits for them, and re-layouts  2.36 us (4%)
  other arithmetic  0.77 us (1%)
  between operations  0.77 us (1%)
    ppermute x2, starting transfers between devices, body(): down = lax.ppermute(piece, 'row', [(i, i + 1) for i in range(3)])  13.3 us
    ppermute x3, waiting for transfers between devices, body(): lax.ppermute(blocks[o], 'row', [(i, (i - o) % n_row) for i in range(n_row)])  7.26 us
    ppermute x3, starting transfers between devices, body(): lax.ppermute(blocks[o], 'row', [(i, (i - o) % n_row) for i in range(n_row)])  6.17 us
    pallas_call x2, Pallas kernels, late_sum(): pl.pallas_call(kernel, in_specs=[SMEM] + [VMEM] * len(operands), out_spec...  4.08 us
    ppermute x2, waiting for transfers between devices, body(): far = lax.ppermute(piece, 'row', [(0, 2), (2, 0), (1, 3), (3, 1)])  3.82 us
    ppermute x2, waiting for transfers between devices, body(): late.append(lax.ppermute(far, 'row', [(2, 3), (1, 0)]))  3.7 us
    ppermute x2, starting transfers between devices, body(): far = lax.ppermute(piece, 'row', [(0, 2), (2, 0), (1, 3), (3, 1)])  3.67 us
    ppermute x1, starting transfers between devices, body(): lax.ppermute(cut[s], 'col', ring_col(s))  3.06 us
  transfers between devices with their start and end apart: 15, of which 8 were waited for; matrix products, arithmetic and copies ran while one was open for 1% of the time, Pallas kernels for 7%

profile of v2, /device:TPU:0, one launch (start us, length us, event | category | flops | bytes accessed | tf_op | source)
XLA Modules:
  0.0 65.3 jit_solution(1955839343645166266)
XLA Ops:
  0.6 0.0 copy-start.4
  0.6 1.1 %cut_columns.1 = (bf16[2,96,512]{2,1,0:T(8,128)(2,1)S(1)}, bf16[2,96,512]{2,1,0:T(8,128)(2,1)S(1)}) custom-call(bf16[2,96,1024]{2,1,0:T(8,128)(2,1)} %bitcast.10), custom_call_target="tpu_custom_call" | custom-call | tf_op jit(solution)/shard_map/cut_columns/pallas_call | solution.py:34
  1.7 3.1 %collective-permute-start.4 = (bf16[2,96,512]{2,1,0:T(8,128)(2,1)S(1)}, bf16[2,96,512]{2,1,0:T(8,128)(2,1)S(1)}, u32[]{:S(2)}, u32[]{:S(2)}) collective-permute-start(bf16[2,96,512]{2,1,0:T(8,128)(2,1)S(1)} %get-tuple-element.12), channel_id=1, source_target_pairs={{0,1},{1,0},{2,3},{3,2},{4,5},{5,4},{6,7},{7,6},{8,9},{9,8},{10,11... | collective-permute-start | bytes 589832 | tf_op jit(solution)/shard_map/ppermute | solution.py:181
  4.8 0.0 copy-start.6
  4.8 2.6 %collective-permute-start.2 = (bf16[2,96,512]{2,1,0:T(8,128)(2,1)S(1)}, bf16[2,96,512]{2,1,0:T(8,128)(2,1)S(1)}, u32[]{:S(2)}, u32[]{:S(2)}) collective-permute-start(bf16[2,96,512]{2,1,0:T(8,128)(2,1)S(1)} %get-tuple-element.11.refs_2_.refs_4_), channel_id=1, source_target_pairs={{0,4},{4,0},{2,6},{6,2},{1,5},{5,1},{3,7},{7,3},{8,12},{12,8},{10,... | collective-permute-start | bytes 589832 | tf_op jit(solution)/shard_map/ppermute | solution.py:187
  7.4 1.3 %collective-permute-start.1 = (bf16[2,96,512]{2,1,0:T(8,128)(2,1)S(1)}, bf16[2,96,512]{2,1,0:T(8,128)(2,1)S(1)}, u32[]{:S(2)}, u32[]{:S(2)}) collective-permute-start(bf16[2,96,512]{2,1,0:T(8,128)(2,1)S(1)} %get-tuple-element.11.refs_2_.refs_4_), channel_id=1, source_target_pairs={{2,0},{4,2},{6,4},{3,1},{5,3},{7,5},{10,8},{12,10},{14,12},{11,9},... | collective-permute-start | bytes 589832 | tf_op jit(solution)/shard_map/ppermute | solution.py:188
  8.7 4.6 %collective-permute-start.3 = (bf16[2,96,512]{2,1,0:T(8,128)(2,1)S(1)}, bf16[2,96,512]{2,1,0:T(8,128)(2,1)S(1)}, u32[]{:S(2)}, u32[]{:S(2)}) collective-permute-start(bf16[2,96,512]{2,1,0:T(8,128)(2,1)S(1)} %get-tuple-element.11.refs_2_.refs_4_), channel_id=1, source_target_pairs={{0,2},{2,4},{4,6},{1,3},{3,5},{5,7},{8,10},{10,12},{12,14},{9,11},... | collective-permute-start | bytes 589832 | tf_op jit(solution)/shard_map/ppermute | solution.py:189
  13.2 0.0 collective-permute-done.4.refs_6_.refs_8_
  13.2 1.1 %collective-permute-start.6 = (bf16[2,96,512]{2,1,0:T(8,128)(2,1)S(1)}, bf16[2,96,512]{2,1,0:T(8,128)(2,1)S(1)}, u32[]{:S(2)}, u32[]{:S(2)}) collective-permute-start(bf16[2,96,512]{2,1,0:T(8,128)(2,1)S(1)} %collective-permute-done.4.refs_6_.refs_8_), channel_id=1, source_target_pairs={{0,4},{4,0},{2,6},{6,2},{1,5},{5,1},{3,7},{7,3},{8,12},{12,8},{10,... | collective-permute-start | bytes 589832 | tf_op jit(solution)/shard_map/ppermute | solution.py:187
  14.3 0.0 copy-done.4
  14.3 0.5 collective-permute-start
  14.8 3.3 %collective-permute-done.2.refs_4_.refs_6_ = bf16[2,96,512]{2,1,0:T(8,128)(2,1)S(1)} collective-permute-done((bf16[2,96,512]{2,1,0:T(8,128)(2,1)S(1)}, bf16[2,96,512]{2,1,0:T(8,128)(2,1)S(1)}, u32[]{:S(2)}, u32[]{:S(2)}) %collective-permute-start.2) | collective-permute-done | bytes 196640 | tf_op jit(solution)/shard_map/ppermute | solution.py:187
  18.2 1.3 %collective-permute-start.5 = (bf16[2,96,512]{2,1,0:T(8,128)(2,1)S(1)}, bf16[2,96,512]{2,1,0:T(8,128)(2,1)S(1)}, u32[]{:S(2)}, u32[]{:S(2)}) collective-permute-start(bf16[2,96,512]{2,1,0:T(8,128)(2,1)S(1)} %collective-permute-done.4.refs_6_.refs_8_), channel_id=1, source_target_pairs={{2,0},{4,2},{6,4},{3,1},{5,3},{7,5},{10,8},{12,10},{14,12},{11,9},... | collective-permute-start | bytes 589832 | tf_op jit(solution)/shard_map/ppermute | solution.py:188
  19.5 0.0 collective-permute-done.1.refs_3_.refs_5_
  19.5 8.8 %collective-permute-start.7 = (bf16[2,96,512]{2,1,0:T(8,128)(2,1)S(1)}, bf16[2,96,512]{2,1,0:T(8,128)(2,1)S(1)}, u32[]{:S(2)}, u32[]{:S(2)}) collective-permute-start(bf16[2,96,512]{2,1,0:T(8,128)(2,1)S(1)} %collective-permute-done.4.refs_6_.refs_8_), channel_id=1, source_target_pairs={{0,2},{2,4},{4,6},{1,3},{3,5},{5,7},{8,10},{10,12},{12,14},{9,11},... | collective-permute-start | bytes 589832 | tf_op jit(solution)/shard_map/ppermute | solution.py:189
  28.3 0.0 collective-permute-done.3.refs_5_.refs_7_
  28.3 1.3 %collective-permute-start.8 = (bf16[2,96,512]{2,1,0:T(8,128)(2,1)S(1)}, bf16[2,96,512]{2,1,0:T(8,128)(2,1)S(1)}, u32[]{:S(2)}, u32[]{:S(2)}) collective-permute-start(bf16[2,96,512]{2,1,0:T(8,128)(2,1)S(1)} %collective-permute-done.2.refs_4_.refs_6_), channel_id=1, source_target_pairs={{4,6},{2,0},{5,7},{3,1},{12,14},{10,8},{13,15},{11,9},{20,22},{18,... | collective-permute-start | bytes 589832 | tf_op jit(solution)/shard_map/ppermute | solution.py:190
  29.6 0.5 collective-permute-done.6.refs_8_.refs_10_
  30.1 1.3 %collective-permute-start.9 = (bf16[2,96,512]{2,1,0:T(8,128)(2,1)S(1)}, bf16[2,96,512]{2,1,0:T(8,128)(2,1)S(1)}, u32[]{:S(2)}, u32[]{:S(2)}) collective-permute-start(bf16[2,96,512]{2,1,0:T(8,128)(2,1)S(1)} %collective-permute-done.6.refs_8_.refs_10_), channel_id=1, source_target_pairs={{4,6},{2,0},{5,7},{3,1},{12,14},{10,8},{13,15},{11,9},{20,22},{18,... | collective-permute-start | bytes 589832 | tf_op jit(solution)/shard_map/ppermute | solution.py:190
  31.3 0.0 copy-done.6
  31.3 0.7 %copy.9.pattern_ref = s32[8,2]{1,0:T(8,128)} copy(s32[8,2]{0,1:T(2,128)S(1)} %copy-done.6) | data formatting | bytes 128 | tf_op args[2]
  32.0 0.0 collective-permute-done.refs_1_
  32.0 0.0 copy-start.5
  32.0 0.0 collective-permute-done.5.refs_7_.refs_9_
  32.0 0.7 %copy-done.5 = bf16[2,4,96,192]{3,2,1,0:T(8,128)(2,1)} copy-done((bf16[2,4,96,192]{3,2,1,0:T(8,128)(2,1)}, bf16[2,4,96,192]{3,2,1,0:T(8,128)(2,1)S(1)}, u32[]{:S(2)}) %copy-start.5) | copy-done | bytes 294936
  32.8 0.0 copy-start
  32.8 0.0 collective-permute-done.7.refs_9_.refs_11_
  32.8 2.3 %early_sum.1.early_ref = f32[2,192,512]{2,1,0:T(8,128)S(1)} custom-call(s32[8,2]{1,0:T(8,128)} %copy.9.pattern_ref, bf16[2,4,96,192]{3,2,1,0:T(8,128)(2,1)} %bitcast.5, bf16[2,4,96,192]{3,2,1,0:T(8,128)(2,1)} %copy-done.5, bf16[2,96,512]{2,1,0:T(8,128)(2,1)S(1)} %get-tuple-element.11.refs_2_.refs_4_, ...), custom_call_target="tpu_custom_call" | custom-call | tf_op jit(solution)/shard_map/early_sum/pallas_call | solution.py:79
  35.1 0.0 copy-done
  35.1 0.0 copy-done.2
  35.1 1.6 %collective-permute-done.8.refs_2_.refs_12_ = bf16[2,96,512]{2,1,0:T(8,128)(2,1)S(1)} collective-permute-done((bf16[2,96,512]{2,1,0:T(8,128)(2,1)S(1)}, bf16[2,96,512]{2,1,0:T(8,128)(2,1)S(1)}, u32[]{:S(2)}, u32[]{:S(2)}) %collective-permute-start.8) | collective-permute-done | bytes 196640 | tf_op jit(solution)/shard_map/ppermute | solution.py:190
  36.7 2.1 %collective-permute-done.9.refs_3_.refs_13_ = bf16[2,96,512]{2,1,0:T(8,128)(2,1)S(1)} collective-permute-done((bf16[2,96,512]{2,1,0:T(8,128)(2,1)S(1)}, bf16[2,96,512]{2,1,0:T(8,128)(2,1)S(1)}, u32[]{:S(2)}, u32[]{:S(2)}) %collective-permute-start.9) | collective-permute-done | bytes 196640 | tf_op jit(solution)/shard_map/ppermute | solution.py:190
  38.8 1.7 %late_sum.1 = (bf16[2,192,128]{2,1,0:T(8,128)(2,1)S(1)}, bf16[2,192,128]{2,1,0:T(8,128)(2,1)S(1)}, bf16[2,192,128]{2,1,0:T(8,128)(2,1)S(1)}, bf16[2,192,128]{2,1,0:T(8,128)(2,1)S(1)}) custom-call(s32[8,2]{1,0:T(8,128)} %copy.9.pattern_ref, f32[2,192,512]{2,1,0:T(8,128)S(1)} %early_sum.1.early_ref, bf16[2,4,96,192]{3,2,1,0:T(8,128)(2,1)} %bitcast.6, ...), custom_call_target="tpu_custom_call" | custom-call | tf_op jit(solution)/shard_map/late_sum/pallas_call | solution.py:114
  40.5 5.5 %collective-permute-start.10 = (bf16[2,192,128]{2,1,0:T(8,128)(2,1)S(1)}, bf16[2,192,128]{2,1,0:T(8,128)(2,1)S(1)}, u32[]{:S(2)}, u32[]{:S(2)}) collective-permute-start(bf16[2,192,128]{2,1,0:T(8,128)(2,1)S(1)} %get-tuple-element.14), channel_id=1, source_target_pairs={{0,6},{2,0},{4,2},{6,4},{1,7},{3,1},{5,3},{7,5},{8,14},{10,8},{12,... | collective-permute-start | bytes 294920 | tf_op jit(solution)/shard_map/ppermute | solution.py:199
  46.0 0.0 collective-permute-start.11
  46.0 0.6 collective-permute-start.12
  46.6 2.5 %collective-permute-done.10.refs_1_ = bf16[2,192,128]{2,1,0:T(8,128)(2,1)S(1)} collective-permute-done((bf16[2,192,128]{2,1,0:T(8,128)(2,1)S(1)}, bf16[2,192,128]{2,1,0:T(8,128)(2,1)S(1)}, u32[]{:S(2)}, u32[]{:S(2)}) %collective-permute-start.10) | collective-permute-done | bytes 98336 | tf_op jit(solution)/shard_map/ppermute | solution.py:199
  49.2 4.7 %collective-permute-done.11.refs_2_ = bf16[2,192,128]{2,1,0:T(8,128)(2,1)S(1)} collective-permute-done((bf16[2,192,128]{2,1,0:T(8,128)(2,1)S(1)}, bf16[2,192,128]{2,1,0:T(8,128)(2,1)S(1)}, u32[]{:S(2)}, u32[]{:S(2)}) %collective-permute-start.11) | collective-permute-done | bytes 98336 | tf_op jit(solution)/shard_map/ppermute | solution.py:199
  53.9 0.0 collective-permute-done.12.refs_3_
  53.9 0.0 copy-done.1
  53.9 0.9 %copy-done.3 = bf16[2,96,512]{2,1,0:T(8,128)(2,1)S(1)} copy-done((bf16[2,96,512]{2,1,0:T(8,128)(2,1)S(1)}, bf16[2,96,512]{2,1,0:T(8,128)(2,1)}, u32[]{:S(2)}) %copy-start.3) | copy-done | bytes 196632
  54.8 2.7 %diagonal.1 = (bf16[2,512,128]{2,1,0:T(8,128)(2,1)}, bf16[512,128]{1,0:T(8,128)(2,1)S(1)}) custom-call(f32[1,2]{1,0:T(1,128)} %weight_ref.1, s32[8,2]{1,0:T(8,128)} %copy.9.pattern_ref, bf16[2,512,128]{2,1,0:T(8,128)(2,1)} %bitcast.11, bf16[2,192,128]{2,1,0:T(8,128)(2,1)S(1)} %get-tuple-element.13.refs_0_, ...), custom_call_target="tpu_custom_call" | custom-call | tf_op jit(solution)/shard_map/diagonal/pallas_call | solution.py:160
  57.6 0.0 collective-permute-start.13
  57.6 1.3 %collective-permute-done.13 = bf16[512,128]{1,0:T(8,128)(2,1)S(1)} collective-permute-done((bf16[512,128]{1,0:T(8,128)(2,1)S(1)}, bf16[512,128]{1,0:T(8,128)(2,1)S(1)}, u32[]{:S(2)}, u32[]{:S(2)}) %collective-permute-start.13) | collective-permute-done | bytes 131104 | tf_op jit(solution)/shard_map/ppermute | solution.py:204
  58.9 1.6 %collective-permute-start.14 = (bf16[512,128]{1,0:T(8,128)(2,1)S(1)}, bf16[512,128]{1,0:T(8,128)(2,1)S(1)}, u32[]{:S(2)}, u32[]{:S(2)}) collective-permute-start(bf16[512,128]{1,0:T(8,128)(2,1)S(1)} %add_convert_fusion), channel_id=1, source_target_pairs={{0,16},{8,24},{16,0},{24,8},{1,17},{9,25},{17,1},{25,9},{2,18},{10... | collective-permute-start | bytes 393224 | tf_op jit(solution)/shard_map/ppermute | solution.py:204
  60.5 2.4 %whole_sum.1 = f32[2,192,512]{2,1,0:T(8,128)} custom-call(s32[8,2]{1,0:T(8,128)} %copy.9.pattern_ref, f32[2,192,512]{2,1,0:T(8,128)S(1)} %early_sum.1.early_ref, bf16[2,4,96,192]{3,2,1,0:T(8,128)(2,1)} %bitcast.7, bf16[2,4,96,192]{3,2,1,0:T(8,128)(2,1)} %copy-done.5, bf16[2,96,512]{2,1,0:T(8,128)(2,1)S(1)} %collective-permute-done.8.refs_2_.refs_12_, ...), custom_call_target="tpu_custom_call" | custom-call | tf_op jit(solution)/shard_map/whole_sum/pallas_call | solution.py:114
  62.9 1.6 %collective-permute-done.14 = bf16[512,128]{1,0:T(8,128)(2,1)S(1)} collective-permute-done((bf16[512,128]{1,0:T(8,128)(2,1)S(1)}, bf16[512,128]{1,0:T(8,128)(2,1)S(1)}, u32[]{:S(2)}, u32[]{:S(2)}) %collective-permute-start.14) | collective-permute-done | bytes 131104 | tf_op jit(solution)/shard_map/ppermute | solution.py:204
  64.6 0.7 %convert_add_fusion = f32[512,128]{1,0:T(8,128)} fusion(bf16[512,128]{1,0:T(8,128)(2,1)S(1)} %collective-permute-done.14, bf16[512,128]{1,0:T(8,128)(2,1)S(1)} %add_convert_fusion), kind=kLoop, calls=%fused_computation | loop fusion | flops 196608 | bytes 524288 | tf_op jit(solution)/shard_map/add | solution.py:205
  (4 shorter events, 0.0 us)
Async XLA Ops:
  0.6 13.7 %copy-start.4 = (bf16[1,2,4,96,192]{4,3,2,1,0:T(8,128)(2,1)S(1)}, bf16[1,2,4,96,192]{4,3,2,1,0:T(8,128)(2,1)}, u32[]{:S(2)}) copy-start(bf16[1,2,4,96,192]{4,3,2,1,0:T(8,128)(2,1)} %param.5) | copy-start | bytes 884740
  1.7 11.5 %collective-permute-start.4 = (bf16[2,96,512]{2,1,0:T(8,128)(2,1)S(1)}, bf16[2,96,512]{2,1,0:T(8,128)(2,1)S(1)}, u32[]{:S(2)}, u32[]{:S(2)}) collective-permute-start(bf16[2,96,512]{2,1,0:T(8,128)(2,1)S(1)} %get-tuple-element.12), channel_id=1, source_target_pairs={{0,1},{1,0},{2,3},{3,2},{4,5},{5,4},{6,7},{7,6},{8,9},{9,8},{10,11... | collective-permute-start | bytes 589832 | tf_op jit(solution)/shard_map/ppermute | solution.py:181
  4.8 26.6 %copy-start.6 = (s32[8,2]{0,1:T(2,128)S(1)}, s32[8,2]{0,1:T(2,128)}, u32[]{:S(2)}) copy-start(s32[8,2]{0,1:T(2,128)} %param.7) | copy-start | bytes 196
  4.8 13.4 %collective-permute-start.2 = (bf16[2,96,512]{2,1,0:T(8,128)(2,1)S(1)}, bf16[2,96,512]{2,1,0:T(8,128)(2,1)S(1)}, u32[]{:S(2)}, u32[]{:S(2)}) collective-permute-start(bf16[2,96,512]{2,1,0:T(8,128)(2,1)S(1)} %get-tuple-element.11.refs_2_.refs_4_), channel_id=1, source_target_pairs={{0,4},{4,0},{2,6},{6,2},{1,5},{5,1},{3,7},{7,3},{8,12},{12,8},{10,... | collective-permute-start | bytes 589832 | tf_op jit(solution)/shard_map/ppermute | solution.py:187
  7.4 12.1 %collective-permute-start.1 = (bf16[2,96,512]{2,1,0:T(8,128)(2,1)S(1)}, bf16[2,96,512]{2,1,0:T(8,128)(2,1)S(1)}, u32[]{:S(2)}, u32[]{:S(2)}) collective-permute-start(bf16[2,96,512]{2,1,0:T(8,128)(2,1)S(1)} %get-tuple-element.11.refs_2_.refs_4_), channel_id=1, source_target_pairs={{2,0},{4,2},{6,4},{3,1},{5,3},{7,5},{10,8},{12,10},{14,12},{11,9},... | collective-permute-start | bytes 589832 | tf_op jit(solution)/shard_map/ppermute | solution.py:188
  8.7 19.6 %collective-permute-start.3 = (bf16[2,96,512]{2,1,0:T(8,128)(2,1)S(1)}, bf16[2,96,512]{2,1,0:T(8,128)(2,1)S(1)}, u32[]{:S(2)}, u32[]{:S(2)}) collective-permute-start(bf16[2,96,512]{2,1,0:T(8,128)(2,1)S(1)} %get-tuple-element.11.refs_2_.refs_4_), channel_id=1, source_target_pairs={{0,2},{2,4},{4,6},{1,3},{3,5},{5,7},{8,10},{10,12},{12,14},{9,11},... | collective-permute-start | bytes 589832 | tf_op jit(solution)/shard_map/ppermute | solution.py:189
  13.2 16.8 %collective-permute-start.6 = (bf16[2,96,512]{2,1,0:T(8,128)(2,1)S(1)}, bf16[2,96,512]{2,1,0:T(8,128)(2,1)S(1)}, u32[]{:S(2)}, u32[]{:S(2)}) collective-permute-start(bf16[2,96,512]{2,1,0:T(8,128)(2,1)S(1)} %collective-permute-done.4.refs_6_.refs_8_), channel_id=1, source_target_pairs={{0,4},{4,0},{2,6},{6,2},{1,5},{5,1},{3,7},{7,3},{8,12},{12,8},{10,... | collective-permute-start | bytes 589832 | tf_op jit(solution)/shard_map/ppermute | solution.py:187
  14.3 17.7 %collective-permute-start = (bf16[2,4,96,192]{3,2,1,0:T(8,128)(2,1)S(1)}, bf16[2,4,96,192]{3,2,1,0:T(8,128)(2,1)S(1)}, u32[]{:S(2)}, u32[]{:S(2)}) collective-permute-start(bf16[2,4,96,192]{3,2,1,0:T(8,128)(2,1)S(1)} %bitcast.8), channel_id=1, source_target_pairs={{0,1},{1,0},{2,3},{3,2},{4,5},{5,4},{6,7},{7,6},{8,9},{9,8},{10,11... | collective-permute-start | bytes 884744 | tf_op jit(solution)/shard_map/ppermute | solution.py:182
  18.2 13.9 %collective-permute-start.5 = (bf16[2,96,512]{2,1,0:T(8,128)(2,1)S(1)}, bf16[2,96,512]{2,1,0:T(8,128)(2,1)S(1)}, u32[]{:S(2)}, u32[]{:S(2)}) collective-permute-start(bf16[2,96,512]{2,1,0:T(8,128)(2,1)S(1)} %collective-permute-done.4.refs_6_.refs_8_), channel_id=1, source_target_pairs={{2,0},{4,2},{6,4},{3,1},{5,3},{7,5},{10,8},{12,10},{14,12},{11,9},... | collective-permute-start | bytes 589832 | tf_op jit(solution)/shard_map/ppermute | solution.py:188
  19.5 13.3 %collective-permute-start.7 = (bf16[2,96,512]{2,1,0:T(8,128)(2,1)S(1)}, bf16[2,96,512]{2,1,0:T(8,128)(2,1)S(1)}, u32[]{:S(2)}, u32[]{:S(2)}) collective-permute-start(bf16[2,96,512]{2,1,0:T(8,128)(2,1)S(1)} %collective-permute-done.4.refs_6_.refs_8_), channel_id=1, source_target_pairs={{0,2},{2,4},{4,6},{1,3},{3,5},{5,7},{8,10},{10,12},{12,14},{9,11},... | collective-permute-start | bytes 589832 | tf_op jit(solution)/shard_map/ppermute | solution.py:189
  28.3 8.4 %collective-permute-start.8 = (bf16[2,96,512]{2,1,0:T(8,128)(2,1)S(1)}, bf16[2,96,512]{2,1,0:T(8,128)(2,1)S(1)}, u32[]{:S(2)}, u32[]{:S(2)}) collective-permute-start(bf16[2,96,512]{2,1,0:T(8,128)(2,1)S(1)} %collective-permute-done.2.refs_4_.refs_6_), channel_id=1, source_target_pairs={{4,6},{2,0},{5,7},{3,1},{12,14},{10,8},{13,15},{11,9},{20,22},{18,... | collective-permute-start | bytes 589832 | tf_op jit(solution)/shard_map/ppermute | solution.py:190
  30.1 8.8 %collective-permute-start.9 = (bf16[2,96,512]{2,1,0:T(8,128)(2,1)S(1)}, bf16[2,96,512]{2,1,0:T(8,128)(2,1)S(1)}, u32[]{:S(2)}, u32[]{:S(2)}) collective-permute-start(bf16[2,96,512]{2,1,0:T(8,128)(2,1)S(1)} %collective-permute-done.6.refs_8_.refs_10_), channel_id=1, source_target_pairs={{4,6},{2,0},{5,7},{3,1},{12,14},{10,8},{13,15},{11,9},{20,22},{18,... | collective-permute-start | bytes 589832 | tf_op jit(solution)/shard_map/ppermute | solution.py:190
  32.0 0.8 %copy-start.5 = (bf16[2,4,96,192]{3,2,1,0:T(8,128)(2,1)}, bf16[2,4,96,192]{3,2,1,0:T(8,128)(2,1)S(1)}, u32[]{:S(2)}) copy-start(bf16[2,4,96,192]{3,2,1,0:T(8,128)(2,1)S(1)} %collective-permute-done.refs_1_) | copy-start | bytes 884740
  32.8 2.3 %copy-start = (bf16[2,96,512]{2,1,0:T(8,128)(2,1)}, bf16[2,96,512]{2,1,0:T(8,128)(2,1)S(1)}, u32[]{:S(2)}) copy-start(bf16[2,96,512]{2,1,0:T(8,128)(2,1)S(1)} %collective-permute-done.5.refs_7_.refs_9_) | copy-start | bytes 589828
  32.8 2.3 %copy-start.2 = (bf16[2,96,512]{2,1,0:T(8,128)(2,1)}, bf16[2,96,512]{2,1,0:T(8,128)(2,1)S(1)}, u32[]{:S(2)}) copy-start(bf16[2,96,512]{2,1,0:T(8,128)(2,1)S(1)} %collective-permute-done.7.refs_9_.refs_11_) | copy-start | bytes 589828
  36.7 17.2 %copy-start.1 = (bf16[2,96,512]{2,1,0:T(8,128)(2,1)S(1)}, bf16[2,96,512]{2,1,0:T(8,128)(2,1)}, u32[]{:S(2)}) copy-start(bf16[2,96,512]{2,1,0:T(8,128)(2,1)} %copy-done) | copy-start | bytes 589828
  40.5 8.7 %collective-permute-start.10 = (bf16[2,192,128]{2,1,0:T(8,128)(2,1)S(1)}, bf16[2,192,128]{2,1,0:T(8,128)(2,1)S(1)}, u32[]{:S(2)}, u32[]{:S(2)}) collective-permute-start(bf16[2,192,128]{2,1,0:T(8,128)(2,1)S(1)} %get-tuple-element.14), channel_id=1, source_target_pairs={{0,6},{2,0},{4,2},{6,4},{1,7},{3,1},{5,3},{7,5},{8,14},{10,8},{12,... | collective-permute-start | bytes 294920 | tf_op jit(solution)/shard_map/ppermute | solution.py:199
  46.0 7.9 %collective-permute-start.11 = (bf16[2,192,128]{2,1,0:T(8,128)(2,1)S(1)}, bf16[2,192,128]{2,1,0:T(8,128)(2,1)S(1)}, u32[]{:S(2)}, u32[]{:S(2)}) collective-permute-start(bf16[2,192,128]{2,1,0:T(8,128)(2,1)S(1)} %get-tuple-element.15), channel_id=1, source_target_pairs={{0,4},{2,6},{4,0},{6,2},{1,5},{3,7},{5,1},{7,3},{8,12},{10,14},{12... | collective-permute-start | bytes 294920 | tf_op jit(solution)/shard_map/ppermute | solution.py:199
  46.0 7.9 %collective-permute-start.12 = (bf16[2,192,128]{2,1,0:T(8,128)(2,1)S(1)}, bf16[2,192,128]{2,1,0:T(8,128)(2,1)S(1)}, u32[]{:S(2)}, u32[]{:S(2)}) collective-permute-start(bf16[2,192,128]{2,1,0:T(8,128)(2,1)S(1)} %get-tuple-element.16), channel_id=1, source_target_pairs={{0,2},{2,4},{4,6},{6,0},{1,3},{3,5},{5,7},{7,1},{8,10},{10,12},{12... | collective-permute-start | bytes 294920 | tf_op jit(solution)/shard_map/ppermute | solution.py:199
  53.9 0.9 %copy-start.3 = (bf16[2,96,512]{2,1,0:T(8,128)(2,1)S(1)}, bf16[2,96,512]{2,1,0:T(8,128)(2,1)}, u32[]{:S(2)}) copy-start(bf16[2,96,512]{2,1,0:T(8,128)(2,1)} %copy-done.2) | copy-start | bytes 589828
  57.6 1.3 %collective-permute-start.13 = (bf16[512,128]{1,0:T(8,128)(2,1)S(1)}, bf16[512,128]{1,0:T(8,128)(2,1)S(1)}, u32[]{:S(2)}, u32[]{:S(2)}) collective-permute-start(bf16[512,128]{1,0:T(8,128)(2,1)S(1)} %get-tuple-element.18), channel_id=1, source_target_pairs={{0,8},{8,0},{16,24},{24,16},{1,9},{9,1},{17,25},{25,17},{2,10},{10... | collective-permute-start | bytes 393224 | tf_op jit(solution)/shard_map/ppermute | solution.py:204
  58.9 5.6 %collective-permute-start.14 = (bf16[512,128]{1,0:T(8,128)(2,1)S(1)}, bf16[512,128]{1,0:T(8,128)(2,1)S(1)}, u32[]{:S(2)}, u32[]{:S(2)}) collective-permute-start(bf16[512,128]{1,0:T(8,128)(2,1)S(1)} %add_convert_fusion), channel_id=1, source_target_pairs={{0,16},{8,24},{16,0},{24,8},{1,17},{9,25},{17,1},{25,9},{2,18},{10... | collective-permute-start | bytes 393224 | tf_op jit(solution)/shard_map/ppermute | solution.py:204

commit v3 on v2

--- a/solution.py
+++ b/solution.py
@@ -10,6 +10,10 @@
     return lax.ppermute(value, axis, [(i, (i + step) % count) for i in range(count)])
 
 
+def named(value, axis, pairs):
+    return lax.ppermute(value, axis, pairs)
+
+
 VMEM = pl.BlockSpec(memory_space=pltpu.VMEM)
 SMEM = pl.BlockSpec(memory_space=pltpu.SMEM)
 
@@ -44,6 +48,10 @@
     col = lax.axis_index("col")
     keep = pattern_ref[q * n_col + lax.rem(col + n_col - s, n_col), col]
     return (block.astype(jnp.float32) * keep.astype(jnp.float32)).astype(jnp.bfloat16)
+
+
+def source_row(row, o, n_row):
+    return row ^ o if n_row == 4 else lax.rem(row + o, n_row)
 
 
 def contract(left, right):
@@ -69,7 +77,7 @@
         sums = None
         for s in range(n_col):
             for o in range(n_row):
-                q = lax.rem(row + o, n_row)
+                q = source_row(row, o, n_row)
                 sums = add_products(pattern_ref, refs[s], q, s, n_col, refs[n_col + s * n_row + o], sums)
         out_ref[0] = sums[0]
         out_ref[1] = sums[1]
@@ -95,7 +103,7 @@
         row = lax.axis_index("row")
         outs = refs[2 * n_late:]
         sums = [early_ref[0], early_ref[1]]
-        q = jnp.where(row == 0, n_row - 1, 0)
+        q = source_row(row, n_row - 1, n_row)
         for s in range(n_late):
             sums = add_products(pattern_ref, refs[s], q, s, n_col, refs[n_late + s], sums)
         if whole:
@@ -106,7 +114,8 @@
         rounded_ref[0] = (-sums[0]).astype(jnp.bfloat16)
         rounded_ref[1] = (-sums[1]).astype(jnp.bfloat16)
         for o in range(n_row):
-            start = pl.multiple_of(lax.rem(row + n_row - o, n_row) * share, 128)
+            target = row ^ o if n_row == 4 else lax.rem(row + n_row - o, n_row)
+            start = pl.multiple_of(target * share, 128)
             outs[o][...] = rounded_ref[:, :, pl.ds(start, share)]
 
     operands = in_vmem([early], near) + (list(segments) + in_vmem(late, near) if late else [])
@@ -139,10 +148,9 @@
         for s in range(n_col):
             start = pl.multiple_of(lax.rem(col + n_col - s, n_col) * block_rows, 16)
             blocks = [ref[:, pl.ds(start, block_rows), :] for ref in half_refs]
-            uses = [(blocks[o], lax.rem(row + o, n_row), piece_refs[s * n_row + o]) for o in range(n_row)]
+            uses = [(blocks[o], source_row(row, o, n_row), piece_refs[s * n_row + o]) for o in range(n_row)]
             if n_late:
-                other = jnp.where(row == 0, blocks[n_row - 1], blocks[1])
-                uses.append((other, jnp.where(row == 0, n_row - 1, 0), late_refs[s]))
+                uses.append((blocks[-1], source_row(row, n_row - 1, n_row), late_refs[s]))
             for half, q, piece_ref in uses:
                 half = kept(half, pattern_ref, q, s, n_col)
                 piece = piece_ref[...].reshape(2 * block_rows, width)
@@ -178,17 +186,17 @@
     near = held <= 3 * 2**20
     cut = cut_columns(panel[0], n_col, width, near)
     ring_col = lambda s: [(i, (i + s) % n_col) for i in range(n_col)]
-    firsts = [cut[0]] + [lax.ppermute(cut[s], "col", ring_col(s)) for s in range(1, n_col)]
-    segments = [anc_inverse[0]] + [lax.ppermute(anc_inverse[0], "col", ring_col(s)) for s in range(1, n_col)]
+    firsts = [cut[0]] + [named(cut[s], "col", ring_col(s)) for s in range(1, n_col)]
+    segments = [anc_inverse[0]] + [named(anc_inverse[0], "col", ring_col(s)) for s in range(1, n_col)]
     pieces = []
     late = []
     for piece in firsts:
         if n_row == 4:
-            far = lax.ppermute(piece, "row", [(0, 2), (2, 0), (1, 3), (3, 1)])
-            up = lax.ppermute(piece, "row", [(i + 1, i) for i in range(3)])
-            down = lax.ppermute(piece, "row", [(i, i + 1) for i in range(3)])
-            late.append(lax.ppermute(far, "row", [(2, 3), (1, 0)]))
-            pieces.append([piece, up, far, down])
+            far = named(piece, "row", [(0, 2), (2, 0), (1, 3), (3, 1)])
+            side = named(piece, "row", [(0, 1), (1, 0), (2, 3), (3, 2)])
+            middle = named(piece, "row", [(1, 2), (2, 1)])
+            late.append(named(far, "row", [(2, 3), (1, 0)]))
+            pieces.append([piece, side, far, middle])
         else:
             pieces.append([piece] + [shift(piece, "row", n_row, -o) for o in range(1, n_row)])
     early = early_sum(pattern, segments, pieces, n_row, near)
@@ -196,7 +204,7 @@
     (result_panel,) = late_sum(pattern, early, segments, late, n_row, True, near)
     halves = [blocks[0]]
     for o in range(1, n_row):
-        halves.append(lax.ppermute(blocks[o], "row", [(i, (i - o) % n_row) for i in range(n_row)]))
+        halves.append(named(blocks[o], "row", [(i, i ^ o if n_row == 4 else (i - o) % n_row) for i in range(n_row)]))
     inv_diag, total = diagonal(pole_weights, pattern, diag_inverse[0], halves, pieces, late, near)
     step = 1
     while step < n_pole:

time: 65.7 us -> 62.1 us (0.945)
  starting transfers between devices: 33.4 us -> 21.5 us
  waiting for transfers between devices: 17.8 us -> 26.3 us
    ppermute x13, starting transfers between devices: 31.9 us -> 19.9 us  [named(): return lax.ppermute(value, axis, pairs)]
    ppermute x13, waiting for transfers between devices: 14.8 us -> 23.3 us  [named(): return lax.ppermute(value, axis, pairs)]
  transfers between devices with their start and end apart: 15 -> 15, of which waited for: 8 -> 8; matrix products, arithmetic and copies ran while one was open for 1% -> 1% of each run, Pallas kernels for 7% -> 8%
where the time goes in v3:
time: 62.1 us; the launch traced here: 61.8 us
  waiting for transfers between devices  26.3 us (42%)
  starting transfers between devices  21.5 us (35%)
  Pallas kernels  10.2 us (16%)
  local copies, waits for them, and re-layouts  2.36 us (4%)
  other arithmetic  0.77 us (1%)
  between operations  0.76 us (1%)
    ppermute x13, waiting for transfers between devices, named(): return lax.ppermute(value, axis, pairs)  23.3 us
    ppermute x13, starting transfers between devices, named(): return lax.ppermute(value, axis, pairs)  19.9 us
    pallas_call x2, Pallas kernels, late_sum(): pl.pallas_call(kernel, in_specs=[SMEM] + [VMEM] * len(operands), out_spec...  4.09 us
    ppermute x2, waiting for transfers between devices, body(): other = lax.ppermute(sent, 'pole', [(i, i ^ step) for i in range(n_pole)])  2.98 us
    pallas_call x1, Pallas kernels, diagonal(): pl.pallas_call(kernel, in_specs=[SMEM, SMEM] + [VMEM] * (1 + len(operands...  2.71 us
    unnamed x15, local copies, waits for them, and re-layouts  2.36 us
    pallas_call x1, Pallas kernels, early_sum(): pl.pallas_call(kernel, in_specs=[SMEM] + [VMEM] * len(operands), out_spec...  2.29 us
    ppermute x2, starting transfers between devices, body(): other = lax.ppermute(sent, 'pole', [(i, i ^ step) for i in range(n_pole)])  1.56 us
  transfers between devices with their start and end apart: 15, of which 8 were waited for; matrix products, arithmetic and copies ran while one was open for 1% of the time, Pallas kernels for 8%

profile of v3, /device:TPU:0, one launch (start us, length us, event | category | flops | bytes accessed | tf_op | source)
XLA Modules:
  0.0 61.8 jit_solution(1053644038782246018)
XLA Ops:
  0.6 0.0 copy-start.4
  0.6 1.1 %cut_columns.1 = (bf16[2,96,512]{2,1,0:T(8,128)(2,1)S(1)}, bf16[2,96,512]{2,1,0:T(8,128)(2,1)S(1)}) custom-call(bf16[2,96,1024]{2,1,0:T(8,128)(2,1)} %bitcast.10), custom_call_target="tpu_custom_call" | custom-call | tf_op jit(solution)/shard_map/cut_columns/pallas_call | solution.py:38
  1.7 3.1 %collective-permute-start.4 = (bf16[2,96,512]{2,1,0:T(8,128)(2,1)S(1)}, bf16[2,96,512]{2,1,0:T(8,128)(2,1)S(1)}, u32[]{:S(2)}, u32[]{:S(2)}) collective-permute-start(bf16[2,96,512]{2,1,0:T(8,128)(2,1)S(1)} %get-tuple-element.12), channel_id=1, source_target_pairs={{0,1},{1,0},{2,3},{3,2},{4,5},{5,4},{6,7},{7,6},{8,9},{9,8},{10,11... | collective-permute-start | bytes 589832 | tf_op jit(solution)/shard_map/ppermute | solution.py:14
  4.8 0.0 copy-start.6
  4.8 2.6 %collective-permute-start.2 = (bf16[2,96,512]{2,1,0:T(8,128)(2,1)S(1)}, bf16[2,96,512]{2,1,0:T(8,128)(2,1)S(1)}, u32[]{:S(2)}, u32[]{:S(2)}) collective-permute-start(bf16[2,96,512]{2,1,0:T(8,128)(2,1)S(1)} %get-tuple-element.11.refs_2_.refs_4_), channel_id=1, source_target_pairs={{0,4},{4,0},{2,6},{6,2},{1,5},{5,1},{3,7},{7,3},{8,12},{12,8},{10,... | collective-permute-start | bytes 589832 | tf_op jit(solution)/shard_map/ppermute | solution.py:14
  7.4 1.6 %collective-permute-start.1 = (bf16[2,96,512]{2,1,0:T(8,128)(2,1)S(1)}, bf16[2,96,512]{2,1,0:T(8,128)(2,1)S(1)}, u32[]{:S(2)}, u32[]{:S(2)}) collective-permute-start(bf16[2,96,512]{2,1,0:T(8,128)(2,1)S(1)} %get-tuple-element.11.refs_2_.refs_4_), channel_id=1, source_target_pairs={{0,2},{2,0},{4,6},{6,4},{1,3},{3,1},{5,7},{7,5},{8,10},{10,8},{12,... | collective-permute-start | bytes 589832 | tf_op jit(solution)/shard_map/ppermute | solution.py:14
  8.9 0.7 %collective-permute-start.3 = (bf16[2,96,512]{2,1,0:T(8,128)(2,1)S(1)}, bf16[2,96,512]{2,1,0:T(8,128)(2,1)S(1)}, u32[]{:S(2)}, u32[]{:S(2)}) collective-permute-start(bf16[2,96,512]{2,1,0:T(8,128)(2,1)S(1)} %get-tuple-element.11.refs_2_.refs_4_), channel_id=1, source_target_pairs={{2,4},{4,2},{3,5},{5,3},{10,12},{12,10},{11,13},{13,11},{18,20},{2... | collective-permute-start | bytes 589832 | tf_op jit(solution)/shard_map/ppermute | solution.py:14
  9.6 0.1 collective-permute-done.4.refs_6_.refs_8_
  9.7 3.2 %collective-permute-start.6 = (bf16[2,96,512]{2,1,0:T(8,128)(2,1)S(1)}, bf16[2,96,512]{2,1,0:T(8,128)(2,1)S(1)}, u32[]{:S(2)}, u32[]{:S(2)}) collective-permute-start(bf16[2,96,512]{2,1,0:T(8,128)(2,1)S(1)} %collective-permute-done.4.refs_6_.refs_8_), channel_id=1, source_target_pairs={{0,4},{4,0},{2,6},{6,2},{1,5},{5,1},{3,7},{7,3},{8,12},{12,8},{10,... | collective-permute-start | bytes 589832 | tf_op jit(solution)/shard_map/ppermute | solution.py:14
  12.8 0.0 copy-done.4
  12.8 1.2 %collective-permute-start = (bf16[2,4,96,192]{3,2,1,0:T(8,128)(2,1)S(1)}, bf16[2,4,96,192]{3,2,1,0:T(8,128)(2,1)S(1)}, u32[]{:S(2)}, u32[]{:S(2)}) collective-permute-start(bf16[2,4,96,192]{3,2,1,0:T(8,128)(2,1)S(1)} %bitcast.8), channel_id=1, source_target_pairs={{0,1},{1,0},{2,3},{3,2},{4,5},{5,4},{6,7},{7,6},{8,9},{9,8},{10,11... | collective-permute-start | bytes 884744 | tf_op jit(solution)/shard_map/ppermute | solution.py:14
  14.0 4.7 %collective-permute-done.2.refs_4_.refs_6_ = bf16[2,96,512]{2,1,0:T(8,128)(2,1)S(1)} collective-permute-done((bf16[2,96,512]{2,1,0:T(8,128)(2,1)S(1)}, bf16[2,96,512]{2,1,0:T(8,128)(2,1)S(1)}, u32[]{:S(2)}, u32[]{:S(2)}) %collective-permute-start.2) | collective-permute-done | bytes 196640 | tf_op jit(solution)/shard_map/ppermute | solution.py:14
  18.7 0.0 collective-permute-start.5
  18.7 0.0 collective-permute-done.1.refs_3_.refs_5_
  18.8 0.7 %collective-permute-start.7 = (bf16[2,96,512]{2,1,0:T(8,128)(2,1)S(1)}, bf16[2,96,512]{2,1,0:T(8,128)(2,1)S(1)}, u32[]{:S(2)}, u32[]{:S(2)}) collective-permute-start(bf16[2,96,512]{2,1,0:T(8,128)(2,1)S(1)} %collective-permute-done.4.refs_6_.refs_8_), channel_id=1, source_target_pairs={{2,4},{4,2},{3,5},{5,3},{10,12},{12,10},{11,13},{13,11},{18,20},{2... | collective-permute-start | bytes 589832 | tf_op jit(solution)/shard_map/ppermute | solution.py:14
  19.4 0.0 collective-permute-done.3.refs_5_.refs_7_
  19.4 1.3 %collective-permute-start.8 = (bf16[2,96,512]{2,1,0:T(8,128)(2,1)S(1)}, bf16[2,96,512]{2,1,0:T(8,128)(2,1)S(1)}, u32[]{:S(2)}, u32[]{:S(2)}) collective-permute-start(bf16[2,96,512]{2,1,0:T(8,128)(2,1)S(1)} %collective-permute-done.2.refs_4_.refs_6_), channel_id=1, source_target_pairs={{4,6},{2,0},{5,7},{3,1},{12,14},{10,8},{13,15},{11,9},{20,22},{18,... | collective-permute-start | bytes 589832 | tf_op jit(solution)/shard_map/ppermute | solution.py:14
  20.7 9.3 %collective-permute-done.6.refs_8_.refs_10_ = bf16[2,96,512]{2,1,0:T(8,128)(2,1)S(1)} collective-permute-done((bf16[2,96,512]{2,1,0:T(8,128)(2,1)S(1)}, bf16[2,96,512]{2,1,0:T(8,128)(2,1)S(1)}, u32[]{:S(2)}, u32[]{:S(2)}) %collective-permute-start.6) | collective-permute-done | bytes 196640 | tf_op jit(solution)/shard_map/ppermute | solution.py:14
  30.0 1.3 %collective-permute-start.9 = (bf16[2,96,512]{2,1,0:T(8,128)(2,1)S(1)}, bf16[2,96,512]{2,1,0:T(8,128)(2,1)S(1)}, u32[]{:S(2)}, u32[]{:S(2)}) collective-permute-start(bf16[2,96,512]{2,1,0:T(8,128)(2,1)S(1)} %collective-permute-done.6.refs_8_.refs_10_), channel_id=1, source_target_pairs={{4,6},{2,0},{5,7},{3,1},{12,14},{10,8},{13,15},{11,9},{20,22},{18,... | collective-permute-start | bytes 589832 | tf_op jit(solution)/shard_map/ppermute | solution.py:14
  31.3 0.0 copy-done.6
  31.3 0.7 %copy.9.pattern_ref = s32[8,2]{1,0:T(8,128)} copy(s32[8,2]{0,1:T(2,128)S(1)} %copy-done.6) | data formatting | bytes 128 | tf_op args[2]
  32.0 0.0 collective-permute-done.refs_1_
  32.0 0.0 copy-start.5
  32.0 0.0 collective-permute-done.5.refs_7_.refs_9_
  32.0 0.7 %copy-done.5 = bf16[2,4,96,192]{3,2,1,0:T(8,128)(2,1)} copy-done((bf16[2,4,96,192]{3,2,1,0:T(8,128)(2,1)}, bf16[2,4,96,192]{3,2,1,0:T(8,128)(2,1)S(1)}, u32[]{:S(2)}) %copy-start.5) | copy-done | bytes 294936
  32.7 0.0 collective-permute-done.7.refs_9_.refs_11_
  32.7 2.3 %early_sum.1.early_ref = f32[2,192,512]{2,1,0:T(8,128)S(1)} custom-call(s32[8,2]{1,0:T(8,128)} %copy.9.pattern_ref, bf16[2,4,96,192]{3,2,1,0:T(8,128)(2,1)} %bitcast.5, bf16[2,4,96,192]{3,2,1,0:T(8,128)(2,1)} %copy-done.5, bf16[2,96,512]{2,1,0:T(8,128)(2,1)S(1)} %get-tuple-element.11.refs_2_.refs_4_, ...), custom_call_target="tpu_custom_call" | custom-call | tf_op jit(solution)/shard_map/early_sum/pallas_call | solution.py:87
  35.0 0.0 copy-done
  35.0 0.0 copy-done.2
  35.0 0.0 collective-permute-done.8.refs_2_.refs_12_
  35.1 0.0 copy-start.1
  35.1 2.5 %collective-permute-done.9.refs_3_.refs_13_ = bf16[2,96,512]{2,1,0:T(8,128)(2,1)S(1)} collective-permute-done((bf16[2,96,512]{2,1,0:T(8,128)(2,1)S(1)}, bf16[2,96,512]{2,1,0:T(8,128)(2,1)S(1)}, u32[]{:S(2)}, u32[]{:S(2)}) %collective-permute-start.9) | collective-permute-done | bytes 196640 | tf_op jit(solution)/shard_map/ppermute | solution.py:14
  37.6 1.7 %late_sum.1 = (bf16[2,192,128]{2,1,0:T(8,128)(2,1)S(1)}, bf16[2,192,128]{2,1,0:T(8,128)(2,1)S(1)}, bf16[2,192,128]{2,1,0:T(8,128)(2,1)S(1)}, bf16[2,192,128]{2,1,0:T(8,128)(2,1)S(1)}) custom-call(s32[8,2]{1,0:T(8,128)} %copy.9.pattern_ref, f32[2,192,512]{2,1,0:T(8,128)S(1)} %early_sum.1.early_ref, bf16[2,4,96,192]{3,2,1,0:T(8,128)(2,1)} %bitcast.6, ...), custom_call_target="tpu_custom_call" | custom-call | tf_op jit(solution)/shard_map/late_sum/pallas_call | solution.py:123
  39.2 0.3 collective-permute-start.10
  39.5 3.9 %collective-permute-start.11 = (bf16[2,192,128]{2,1,0:T(8,128)(2,1)S(1)}, bf16[2,192,128]{2,1,0:T(8,128)(2,1)S(1)}, u32[]{:S(2)}, u32[]{:S(2)}) collective-permute-start(bf16[2,192,128]{2,1,0:T(8,128)(2,1)S(1)} %get-tuple-element.15), channel_id=1, source_target_pairs={{0,4},{2,6},{4,0},{6,2},{1,5},{3,7},{5,1},{7,3},{8,12},{10,14},{12... | collective-permute-start | bytes 294920 | tf_op jit(solution)/shard_map/ppermute | solution.py:14
  43.4 0.3 collective-permute-start.12
  43.7 1.3 %collective-permute-done.10.refs_1_ = bf16[2,192,128]{2,1,0:T(8,128)(2,1)S(1)} collective-permute-done((bf16[2,192,128]{2,1,0:T(8,128)(2,1)S(1)}, bf16[2,192,128]{2,1,0:T(8,128)(2,1)S(1)}, u32[]{:S(2)}, u32[]{:S(2)}) %collective-permute-start.10) | collective-permute-done | bytes 98336 | tf_op jit(solution)/shard_map/ppermute | solution.py:14
  45.0 5.4 %collective-permute-done.11.refs_2_ = bf16[2,192,128]{2,1,0:T(8,128)(2,1)S(1)} collective-permute-done((bf16[2,192,128]{2,1,0:T(8,128)(2,1)S(1)}, bf16[2,192,128]{2,1,0:T(8,128)(2,1)S(1)}, u32[]{:S(2)}, u32[]{:S(2)}) %collective-permute-start.11) | collective-permute-done | bytes 98336 | tf_op jit(solution)/shard_map/ppermute | solution.py:14
  50.4 0.0 collective-permute-done.12.refs_3_
  50.4 0.0 copy-done.1
  50.4 0.9 %copy-done.3 = bf16[2,96,512]{2,1,0:T(8,128)(2,1)S(1)} copy-done((bf16[2,96,512]{2,1,0:T(8,128)(2,1)S(1)}, bf16[2,96,512]{2,1,0:T(8,128)(2,1)}, u32[]{:S(2)}) %copy-start.3) | copy-done | bytes 196632
  51.3 2.7 %diagonal.1 = (bf16[2,512,128]{2,1,0:T(8,128)(2,1)}, bf16[512,128]{1,0:T(8,128)(2,1)S(1)}) custom-call(f32[1,2]{1,0:T(1,128)} %weight_ref.1, s32[8,2]{1,0:T(8,128)} %copy.9.pattern_ref, bf16[2,512,128]{2,1,0:T(8,128)(2,1)} %bitcast.11, bf16[2,192,128]{2,1,0:T(8,128)(2,1)S(1)} %get-tuple-element.13.refs_0_, ...), custom_call_target="tpu_custom_call" | custom-call | tf_op jit(solution)/shard_map/diagonal/pallas_call | solution.py:168
  54.0 0.0 collective-permute-start.13
  54.1 1.3 %collective-permute-done.13 = bf16[512,128]{1,0:T(8,128)(2,1)S(1)} collective-permute-done((bf16[512,128]{1,0:T(8,128)(2,1)S(1)}, bf16[512,128]{1,0:T(8,128)(2,1)S(1)}, u32[]{:S(2)}, u32[]{:S(2)}) %collective-permute-start.13) | collective-permute-done | bytes 131104 | tf_op jit(solution)/shard_map/ppermute | solution.py:212
  55.4 1.6 %collective-permute-start.14 = (bf16[512,128]{1,0:T(8,128)(2,1)S(1)}, bf16[512,128]{1,0:T(8,128)(2,1)S(1)}, u32[]{:S(2)}, u32[]{:S(2)}) collective-permute-start(bf16[512,128]{1,0:T(8,128)(2,1)S(1)} %add_convert_fusion), channel_id=1, source_target_pairs={{0,16},{8,24},{16,0},{24,8},{1,17},{9,25},{17,1},{25,9},{2,18},{10... | collective-permute-start | bytes 393224 | tf_op jit(solution)/shard_map/ppermute | solution.py:212
  57.0 2.4 %whole_sum.1 = f32[2,192,512]{2,1,0:T(8,128)} custom-call(s32[8,2]{1,0:T(8,128)} %copy.9.pattern_ref, f32[2,192,512]{2,1,0:T(8,128)S(1)} %early_sum.1.early_ref, bf16[2,4,96,192]{3,2,1,0:T(8,128)(2,1)} %bitcast.7, bf16[2,4,96,192]{3,2,1,0:T(8,128)(2,1)} %copy-done.5, bf16[2,96,512]{2,1,0:T(8,128)(2,1)S(1)} %collective-permute-done.8.refs_2_.refs_12_, ...), custom_call_target="tpu_custom_call" | custom-call | tf_op jit(solution)/shard_map/whole_sum/pallas_call | solution.py:123
  59.4 1.6 %collective-permute-done.14 = bf16[512,128]{1,0:T(8,128)(2,1)S(1)} collective-permute-done((bf16[512,128]{1,0:T(8,128)(2,1)S(1)}, bf16[512,128]{1,0:T(8,128)(2,1)S(1)}, u32[]{:S(2)}, u32[]{:S(2)}) %collective-permute-start.14) | collective-permute-done | bytes 131104 | tf_op jit(solution)/shard_map/ppermute | solution.py:212
  61.1 0.7 %convert_add_fusion = f32[512,128]{1,0:T(8,128)} fusion(bf16[512,128]{1,0:T(8,128)(2,1)S(1)} %collective-permute-done.14, bf16[512,128]{1,0:T(8,128)(2,1)S(1)} %add_convert_fusion), kind=kLoop, calls=%fused_computation | loop fusion | flops 196608 | bytes 524288 | tf_op jit(solution)/shard_map/add | solution.py:213
  (4 shorter events, 0.0 us)
Async XLA Ops:
  0.6 12.2 %copy-start.4 = (bf16[1,2,4,96,192]{4,3,2,1,0:T(8,128)(2,1)S(1)}, bf16[1,2,4,96,192]{4,3,2,1,0:T(8,128)(2,1)}, u32[]{:S(2)}) copy-start(bf16[1,2,4,96,192]{4,3,2,1,0:T(8,128)(2,1)} %param.5) | copy-start | bytes 884740
  1.7 8.0 %collective-permute-start.4 = (bf16[2,96,512]{2,1,0:T(8,128)(2,1)S(1)}, bf16[2,96,512]{2,1,0:T(8,128)(2,1)S(1)}, u32[]{:S(2)}, u32[]{:S(2)}) collective-permute-start(bf16[2,96,512]{2,1,0:T(8,128)(2,1)S(1)} %get-tuple-element.12), channel_id=1, source_target_pairs={{0,1},{1,0},{2,3},{3,2},{4,5},{5,4},{6,7},{7,6},{8,9},{9,8},{10,11... | collective-permute-start | bytes 589832 | tf_op jit(solution)/shard_map/ppermute | solution.py:14
  4.8 26.5 %copy-start.6 = (s32[8,2]{0,1:T(2,128)S(1)}, s32[8,2]{0,1:T(2,128)}, u32[]{:S(2)}) copy-start(s32[8,2]{0,1:T(2,128)} %param.7) | copy-start | bytes 196
  4.8 14.0 %collective-permute-start.2 = (bf16[2,96,512]{2,1,0:T(8,128)(2,1)S(1)}, bf16[2,96,512]{2,1,0:T(8,128)(2,1)S(1)}, u32[]{:S(2)}, u32[]{:S(2)}) collective-permute-start(bf16[2,96,512]{2,1,0:T(8,128)(2,1)S(1)} %get-tuple-element.11.refs_2_.refs_4_), channel_id=1, source_target_pairs={{0,4},{4,0},{2,6},{6,2},{1,5},{5,1},{3,7},{7,3},{8,12},{12,8},{10,... | collective-permute-start | bytes 589832 | tf_op jit(solution)/shard_map/ppermute | solution.py:14
  7.4 11.4 %collective-permute-start.1 = (bf16[2,96,512]{2,1,0:T(8,128)(2,1)S(1)}, bf16[2,96,512]{2,1,0:T(8,128)(2,1)S(1)}, u32[]{:S(2)}, u32[]{:S(2)}) collective-permute-start(bf16[2,96,512]{2,1,0:T(8,128)(2,1)S(1)} %get-tuple-element.11.refs_2_.refs_4_), channel_id=1, source_target_pairs={{0,2},{2,0},{4,6},{6,4},{1,3},{3,1},{5,7},{7,5},{8,10},{10,8},{12,... | collective-permute-start | bytes 589832 | tf_op jit(solution)/shard_map/ppermute | solution.py:14
  8.9 10.5 %collective-permute-start.3 = (bf16[2,96,512]{2,1,0:T(8,128)(2,1)S(1)}, bf16[2,96,512]{2,1,0:T(8,128)(2,1)S(1)}, u32[]{:S(2)}, u32[]{:S(2)}) collective-permute-start(bf16[2,96,512]{2,1,0:T(8,128)(2,1)S(1)} %get-tuple-element.11.refs_2_.refs_4_), channel_id=1, source_target_pairs={{2,4},{4,2},{3,5},{5,3},{10,12},{12,10},{11,13},{13,11},{18,20},{2... | collective-permute-start | bytes 589832 | tf_op jit(solution)/shard_map/ppermute | solution.py:14
  9.7 20.3 %collective-permute-start.6 = (bf16[2,96,512]{2,1,0:T(8,128)(2,1)S(1)}, bf16[2,96,512]{2,1,0:T(8,128)(2,1)S(1)}, u32[]{:S(2)}, u32[]{:S(2)}) collective-permute-start(bf16[2,96,512]{2,1,0:T(8,128)(2,1)S(1)} %collective-permute-done.4.refs_6_.refs_8_), channel_id=1, source_target_pairs={{0,4},{4,0},{2,6},{6,2},{1,5},{5,1},{3,7},{7,3},{8,12},{12,8},{10,... | collective-permute-start | bytes 589832 | tf_op jit(solution)/shard_map/ppermute | solution.py:14
  12.8 19.1 %collective-permute-start = (bf16[2,4,96,192]{3,2,1,0:T(8,128)(2,1)S(1)}, bf16[2,4,96,192]{3,2,1,0:T(8,128)(2,1)S(1)}, u32[]{:S(2)}, u32[]{:S(2)}) collective-permute-start(bf16[2,4,96,192]{3,2,1,0:T(8,128)(2,1)S(1)} %bitcast.8), channel_id=1, source_target_pairs={{0,1},{1,0},{2,3},{3,2},{4,5},{5,4},{6,7},{7,6},{8,9},{9,8},{10,11... | collective-permute-start | bytes 884744 | tf_op jit(solution)/shard_map/ppermute | solution.py:14
  18.7 13.2 %collective-permute-start.5 = (bf16[2,96,512]{2,1,0:T(8,128)(2,1)S(1)}, bf16[2,96,512]{2,1,0:T(8,128)(2,1)S(1)}, u32[]{:S(2)}, u32[]{:S(2)}) collective-permute-start(bf16[2,96,512]{2,1,0:T(8,128)(2,1)S(1)} %collective-permute-done.4.refs_6_.refs_8_), channel_id=1, source_target_pairs={{0,2},{2,0},{4,6},{6,4},{1,3},{3,1},{5,7},{7,5},{8,10},{10,8},{12,... | collective-permute-start | bytes 589832 | tf_op jit(solution)/shard_map/ppermute | solution.py:14
  18.8 14.0 %collective-permute-start.7 = (bf16[2,96,512]{2,1,0:T(8,128)(2,1)S(1)}, bf16[2,96,512]{2,1,0:T(8,128)(2,1)S(1)}, u32[]{:S(2)}, u32[]{:S(2)}) collective-permute-start(bf16[2,96,512]{2,1,0:T(8,128)(2,1)S(1)} %collective-permute-done.4.refs_6_.refs_8_), channel_id=1, source_target_pairs={{2,4},{4,2},{3,5},{5,3},{10,12},{12,10},{11,13},{13,11},{18,20},{2... | collective-permute-start | bytes 589832 | tf_op jit(solution)/shard_map/ppermute | solution.py:14
  19.4 15.6 %collective-permute-start.8 = (bf16[2,96,512]{2,1,0:T(8,128)(2,1)S(1)}, bf16[2,96,512]{2,1,0:T(8,128)(2,1)S(1)}, u32[]{:S(2)}, u32[]{:S(2)}) collective-permute-start(bf16[2,96,512]{2,1,0:T(8,128)(2,1)S(1)} %collective-permute-done.2.refs_4_.refs_6_), channel_id=1, source_target_pairs={{4,6},{2,0},{5,7},{3,1},{12,14},{10,8},{13,15},{11,9},{20,22},{18,... | collective-permute-start | bytes 589832 | tf_op jit(solution)/shard_map/ppermute | solution.py:14
  30.0 7.6 %collective-permute-start.9 = (bf16[2,96,512]{2,1,0:T(8,128)(2,1)S(1)}, bf16[2,96,512]{2,1,0:T(8,128)(2,1)S(1)}, u32[]{:S(2)}, u32[]{:S(2)}) collective-permute-start(bf16[2,96,512]{2,1,0:T(8,128)(2,1)S(1)} %collective-permute-done.6.refs_8_.refs_10_), channel_id=1, source_target_pairs={{4,6},{2,0},{5,7},{3,1},{12,14},{10,8},{13,15},{11,9},{20,22},{18,... | collective-permute-start | bytes 589832 | tf_op jit(solution)/shard_map/ppermute | solution.py:14
  32.0 0.8 %copy-start.5 = (bf16[2,4,96,192]{3,2,1,0:T(8,128)(2,1)}, bf16[2,4,96,192]{3,2,1,0:T(8,128)(2,1)S(1)}, u32[]{:S(2)}) copy-start(bf16[2,4,96,192]{3,2,1,0:T(8,128)(2,1)S(1)} %collective-permute-done.refs_1_) | copy-start | bytes 884740
  32.7 2.3 %copy-start = (bf16[2,96,512]{2,1,0:T(8,128)(2,1)}, bf16[2,96,512]{2,1,0:T(8,128)(2,1)S(1)}, u32[]{:S(2)}) copy-start(bf16[2,96,512]{2,1,0:T(8,128)(2,1)S(1)} %collective-permute-done.5.refs_7_.refs_9_) | copy-start | bytes 589828
  32.7 2.3 %copy-start.2 = (bf16[2,96,512]{2,1,0:T(8,128)(2,1)}, bf16[2,96,512]{2,1,0:T(8,128)(2,1)S(1)}, u32[]{:S(2)}) copy-start(bf16[2,96,512]{2,1,0:T(8,128)(2,1)S(1)} %collective-permute-done.7.refs_9_.refs_11_) | copy-start | bytes 589828
  35.1 15.3 %copy-start.1 = (bf16[2,96,512]{2,1,0:T(8,128)(2,1)S(1)}, bf16[2,96,512]{2,1,0:T(8,128)(2,1)}, u32[]{:S(2)}) copy-start(bf16[2,96,512]{2,1,0:T(8,128)(2,1)} %copy-done) | copy-start | bytes 589828
  39.2 5.7 %collective-permute-start.10 = (bf16[2,192,128]{2,1,0:T(8,128)(2,1)S(1)}, bf16[2,192,128]{2,1,0:T(8,128)(2,1)S(1)}, u32[]{:S(2)}, u32[]{:S(2)}) collective-permute-start(bf16[2,192,128]{2,1,0:T(8,128)(2,1)S(1)} %get-tuple-element.14), channel_id=1, source_target_pairs={{0,2},{2,0},{4,6},{6,4},{1,3},{3,1},{5,7},{7,5},{8,10},{10,8},{12,... | collective-permute-start | bytes 294920 | tf_op jit(solution)/shard_map/ppermute | solution.py:14
  39.5 10.9 %collective-permute-start.11 = (bf16[2,192,128]{2,1,0:T(8,128)(2,1)S(1)}, bf16[2,192,128]{2,1,0:T(8,128)(2,1)S(1)}, u32[]{:S(2)}, u32[]{:S(2)}) collective-permute-start(bf16[2,192,128]{2,1,0:T(8,128)(2,1)S(1)} %get-tuple-element.15), channel_id=1, source_target_pairs={{0,4},{2,6},{4,0},{6,2},{1,5},{3,7},{5,1},{7,3},{8,12},{10,14},{12... | collective-permute-start | bytes 294920 | tf_op jit(solution)/shard_map/ppermute | solution.py:14
  43.4 7.0 %collective-permute-start.12 = (bf16[2,192,128]{2,1,0:T(8,128)(2,1)S(1)}, bf16[2,192,128]{2,1,0:T(8,128)(2,1)S(1)}, u32[]{:S(2)}, u32[]{:S(2)}) collective-permute-start(bf16[2,192,128]{2,1,0:T(8,128)(2,1)S(1)} %get-tuple-element.16), channel_id=1, source_target_pairs={{0,6},{2,4},{4,2},{6,0},{1,7},{3,5},{5,3},{7,1},{8,14},{10,12},{12... | collective-permute-start | bytes 294920 | tf_op jit(solution)/shard_map/ppermute | solution.py:14
  50.4 0.9 %copy-start.3 = (bf16[2,96,512]{2,1,0:T(8,128)(2,1)S(1)}, bf16[2,96,512]{2,1,0:T(8,128)(2,1)}, u32[]{:S(2)}) copy-start(bf16[2,96,512]{2,1,0:T(8,128)(2,1)} %copy-done.2) | copy-start | bytes 589828
  54.0 1.3 %collective-permute-start.13 = (bf16[512,128]{1,0:T(8,128)(2,1)S(1)}, bf16[512,128]{1,0:T(8,128)(2,1)S(1)}, u32[]{:S(2)}, u32[]{:S(2)}) collective-permute-start(bf16[512,128]{1,0:T(8,128)(2,1)S(1)} %get-tuple-element.18), channel_id=1, source_target_pairs={{0,8},{8,0},{16,24},{24,16},{1,9},{9,1},{17,25},{25,17},{2,10},{10... | collective-permute-start | bytes 393224 | tf_op jit(solution)/shard_map/ppermute | solution.py:212
  55.4 5.6 %collective-permute-start.14 = (bf16[512,128]{1,0:T(8,128)(2,1)S(1)}, bf16[512,128]{1,0:T(8,128)(2,1)S(1)}, u32[]{:S(2)}, u32[]{:S(2)}) collective-permute-start(bf16[512,128]{1,0:T(8,128)(2,1)S(1)} %add_convert_fusion), channel_id=1, source_target_pairs={{0,16},{8,24},{16,0},{24,8},{1,17},{9,25},{17,1},{25,9},{2,18},{10... | collective-permute-start | bytes 393224 | tf_op jit(solution)/shard_map/ppermute | solution.py:212
